TPU v7x, 512 devices: a whole 4x8x8 slice. The times are simulated.
512 devices in a mesh: seq: 64 (over z_hi, x, y), head: 8 (over z_lo, core).
Axes of the slice: x: 4, y: 8, z: 8 (z_hi: 2, z_lo: 4; z = z_hi * 4 + z_lo), core: 2. Of those that a mesh axis runs over, the one named last changes fastest.
Arguments:
- queries: bfloat16 [12288, 32, 128], P('seq', 'head'), may hold values from -180 to 180
- key_rows: bfloat16 [12288, 8, 128], P('seq', 'head'), may hold values from -4.5 to 4.5
- value_rows: bfloat16 [12288, 8, 128], P('seq', 'head'), may hold values from -24 to 24
- windows: int32 [32], P('head'), may hold values from 768 to 1536, as said below
- sink_counts: int32 [32], P('head'), may hold values from 1 to 4, as said below
- sink_bias: float32 [32], P('head'), may hold values from 3 to 7
- out_weight: bfloat16 [4096, 4096], P('head'), may hold values from -0.09375 to 0.09375
Outputs:
- attn_out: bfloat16 [12288, 4096], P(('seq', 'head'))
Inputs may be any that keep to these rules, and one draw needn't show every extreme that they name: `windows`: each head's window lies between 768 and 1536, and some head has exactly 1536. `sink_counts`: each head has 1 to 4 sink tokens, and some head has exactly 4.
All inputs are finite; a program needn't handle non-finite values.
Results may differ from a plain program's by a relative error of at most 0.018.
Values may be sent and summed in bfloat16 or wider, within the bound.
No kernel may reach another device: no remote copies, remote signals or barrier semaphores. Data moves between devices by JAX's collectives and lax.ppermute only.
A program may use at most 64 MiB of HBM per device.

v0:
```python
import functools

import jax
import jax.numpy as jnp
from jax import lax
from jax.experimental import pallas as pl
from jax.experimental.pallas import tpu as pltpu
from jax.sharding import Mesh
from jax.sharding import PartitionSpec as P

SINKS = 4
SEQ = ("zh", "x", "y")
HEAD = ("zl", "core")
LANES = 128
NEG = -1e30
LOG2E = 1.4426950408889634
SPREAD = (
    (SEQ, [(0, 32)]),
    (SEQ, [(i, i + 8) for i in (0, 32)]),
    (SEQ, [(i, i + j) for i in (0, 32) for i, j in ((i, 24), (i + 8, 8))]),
    ("y", [(0, 1)]),
    ("y", [(0, 7), (1, 2)]),
    ("y", [(7, 5), (0, 6), (1, 3), (2, 4)]),
)
ORDER = (4, 5, 6, 7, 3, 2, 1, 0)
ALWAYS, NEVER = 1 << 30, -(1 << 30)


def listed(number):
    return sum(jnp.where(number == k, y, 0) for k, y in enumerate(ORDER))


def pack_kernel(y_ref, own_ref, before_ref, sent_ref):
    target = listed(lax.broadcasted_iota(jnp.int32, y_ref.shape, 0))
    later = (target > y_ref[...]).astype(jnp.float32).astype(jnp.bfloat16)
    for number in range(sent_ref.shape[0]):
        chosen = later[number : number + 1]
        sent_ref[number] = own_ref[...] * chosen + before_ref[...] * (1 - chosen)


def pack(y, own, before, row_len):
    vmem = pl.BlockSpec(memory_space=pltpu.VMEM)
    return pl.pallas_call(
        pack_kernel,
        out_shape=jax.ShapeDtypeStruct((row_len, *own.shape), own.dtype),
        in_specs=[vmem] * 3,
        out_specs=vmem,
        compiler_params=pltpu.CompilerParams(vmem_limit_bytes=8 << 20),
        name="pack",
    )(jnp.full((row_len, LANES), y, jnp.int32), own, before)


def attend_kernel(
    table, bias, q_ref, halo_ref, near_ref, out_ref, score_ref, prob_ref, *, tok_rows, number
):
    heads, rows, width = q_ref.shape[1:]
    first_pos, y, member, part = (table[k : k + 1, :1] for k in (0, 1, 2, 3 + number))
    unit = LOG2E / width**0.5
    halo_len = halo_ref.shape[0] * tok_rows
    span = score_ref.shape[1]
    per = rows // 4
    row = lax.broadcasted_iota(jnp.int32, (rows, 1), 0)
    turn = sum((row >= per * k).astype(jnp.int32) for k in range(1, 4))
    query_pos = first_pos + (turn ^ member) * (2 * per) + part * per + row - turn * per
    place = lax.broadcasted_iota(jnp.int32, (1, halo_len), 1)
    block = sum((place >= k * tok_rows).astype(jnp.int32) for k in range(1, len(ORDER)))
    source = listed(block)
    halo_pos = first_pos + (source - y - block) * tok_rows + place
    halo_pos = halo_pos - jnp.where(source < y, 0, halo_len)
    near = lax.broadcasted_iota(jnp.int32, (1, span - halo_len), 1)
    is_sink = near >= tok_rows
    near_pos = jnp.where(is_sink, near - tok_rows, first_pos + near)
    first = (1 - part).astype(jnp.float32).astype(jnp.bfloat16)
    q = (q_ref[0] * first + q_ref[1] * (1 - first)).reshape(heads * rows, width)
    transposed = (((1,), (1,)), ((), ()))
    keys = jnp.concatenate([halo_ref[:, 0].reshape(halo_len, width), near_ref[0]], axis=0)
    score_ref[...] = lax.dot_general(q, keys, transposed, preferred_element_type=jnp.float32)
    totals = []
    for h in range(heads):
        window, count = (table[k : k + 1, :1] for k in (5 + h, 5 + heads + h))
        lowest = jnp.maximum(query_pos - window + 1, count)
        ranked = jnp.where(is_sink, jnp.where(near_pos < count, ALWAYS, NEVER), near_pos)
        mine = slice(h * rows, (h + 1) * rows)
        far = jnp.where(halo_pos >= lowest, score_ref[mine, :halo_len], NEG)
        close = score_ref[mine, halo_len:] + jnp.where(is_sink, bias[h : h + 1, :1], 0.0)
        close = jnp.where((near_pos <= query_pos) & (ranked >= lowest), close, NEG)
        top = jnp.maximum(
            jnp.max(far, axis=1, keepdims=True), jnp.max(close, axis=1, keepdims=True)
        )
        far = jnp.exp2((far - top) * unit)
        close = jnp.exp2((close - top) * unit)
        totals.append(jnp.sum(far, axis=1, keepdims=True) + jnp.sum(close, axis=1, keepdims=True))
        prob_ref[mine, :halo_len] = far.astype(jnp.bfloat16)
        prob_ref[mine, halo_len:] = close.astype(jnp.bfloat16)
    values = jnp.concatenate([halo_ref[:, 1].reshape(halo_len, width), near_ref[1]], axis=0)
    mixed = jnp.dot(prob_ref[...], values, preferred_element_type=jnp.float32)
    for h in range(heads):
        block = mixed[h * rows : (h + 1) * rows] / totals[h]
        out_ref[:, h * width : (h + 1) * width] = block.astype(out_ref.dtype)


def attend(number, table, sink_bias, q, halo, near):
    heads, rows, width = q.shape[1:]
    tok_rows = halo.shape[2]
    vmem = pl.BlockSpec(memory_space=pltpu.VMEM)
    span = halo.shape[0] * tok_rows + near.shape[1]
    return pl.pallas_call(
        functools.partial(attend_kernel, tok_rows=tok_rows, number=number),
        out_shape=jax.ShapeDtypeStruct((rows, heads * width), jnp.bfloat16),
        in_specs=[vmem] * 5,
        out_specs=vmem,
        scratch_shapes=[
            pltpu.VMEM((heads * rows, span), jnp.float32),
            pltpu.VMEM((heads * rows, span), jnp.bfloat16),
        ],
        cost_estimate=pl.CostEstimate(
            flops=32 * heads * rows * span * width,
            bytes_accessed=halo.size * 2,
            transcendentals=heads * rows * span,
        ),
        compiler_params=pltpu.CompilerParams(vmem_limit_bytes=20 << 20),
        name="attend",
    )(table, sink_bias, q, halo, near)


def project_kernel(rows_ref, weight_ref, theirs_ref, *out_refs):
    per = out_refs[0].shape[0]
    step = 512

    for k in range(weight_ref.shape[1] // step):
        columns = slice(k * step, (k + 1) * step)
        total = jnp.dot(rows_ref[...], weight_ref[:, columns], preferred_element_type=jnp.float32)
        total = total.astype(jnp.bfloat16).astype(jnp.float32)
        total = total + theirs_ref[:, columns].astype(jnp.float32)
        for number, out_ref in enumerate(out_refs):
            out_ref[:, columns] = total[number * per : (number + 1) * per].astype(out_ref.dtype)


def project(rows, weight, theirs, members):
    vmem = pl.BlockSpec(memory_space=pltpu.VMEM)
    per, columns = rows.shape[0] // members, weight.shape[1]
    return pl.pallas_call(
        project_kernel,
        out_shape=[jax.ShapeDtypeStruct((per, columns), jnp.bfloat16)] * members,
        in_specs=[vmem] * 3,
        out_specs=[vmem] * members,
        cost_estimate=pl.CostEstimate(
            flops=2 * rows.size * columns, bytes_accessed=weight.size * 2, transcendentals=0
        ),
        compiler_params=pltpu.CompilerParams(vmem_limit_bytes=20 << 20),
        name="project",
    )(rows, weight, theirs)


def shards(queries, key_rows, value_rows, windows, sink_counts, sink_bias, out_weight):
    tok_rows, heads, width = queries.shape
    row_len = lax.axis_size("y")
    seq_len = lax.axis_size(SEQ)
    y, core = lax.axis_index("y"), lax.axis_index("core")
    first_pos = lax.axis_index(SEQ) * tok_rows
    stacked = jnp.stack([key_rows[:, 0], value_rows[:, 0]])
    before = lax.ppermute(stacked, SEQ, [(i, i + row_len) for i in range(seq_len - row_len)])
    sinks = jnp.where(lax.axis_index(SEQ) == 0, stacked[:, :SINKS], 0)
    moved = lax.ppermute(sinks, *SPREAD[0])
    sent = pack(y, stacked, before, row_len)
    halo = lax.all_to_all(sent, "y", 0, 0, axis_index_groups=[list(ORDER)], tiled=True)
    sinks, moved, windows, sink_counts, sink_bias, _ = lax.optimization_barrier(
        (sinks, moved, windows, sink_counts, sink_bias, sent)
    )
    sinks = sinks + moved
    for number, (axis, route) in enumerate(SPREAD[1:], 1):
        if number == len(SPREAD) - 1:
            sinks, queries = lax.optimization_barrier((sinks, queries))
        sinks = sinks + lax.ppermute(sinks, axis, route)
    near = jnp.concatenate(
        [stacked, jnp.pad(sinks, ((0, 0), (0, 64 - SINKS), (0, 0)))], axis=1
    )
    members, cores = lax.axis_size("zl"), lax.axis_size("core")
    own = tok_rows // (members * cores)
    member = lax.axis_index("zl")
    q = queries.reshape(2, 2, cores, own, heads, width)
    q = jnp.where(member % 2 == 1, jnp.stack([q[:, 1], q[:, 0]], axis=1), q)
    q = jnp.where(member // 2 == 1, jnp.stack([q[1], q[0]]), q)
    q = q.reshape(members, cores, own, heads, width)
    q = q.transpose(1, 3, 0, 2, 4).reshape(cores, heads, members * own, width)
    place = jnp.stack([first_pos, y, member, 1 - core, core]).astype(jnp.int32)
    table = jnp.concatenate([place, windows, sink_counts])
    table = jnp.pad(table, (0, -len(table) % 8))[:, None]
    bias = jnp.pad(sink_bias * width**0.5, (0, 8 - heads))[:, None]
    table = jnp.broadcast_to(table, (16, LANES))
    bias = jnp.broadcast_to(bias, (8, LANES))
    theirs = attend(0, table, bias, q, halo, near)
    theirs = jnp.dot(theirs, out_weight, preferred_element_type=jnp.float32).astype(jnp.bfloat16)
    theirs = lax.ppermute(theirs, "core", [(0, 1), (1, 0)])
    mine = attend(1, table, bias, q, halo, near)
    parts = project(mine, out_weight, theirs, members)
    total = parts[0].astype(jnp.float32)
    for distance in (3, 2, 1):
        route = [(i, i ^ distance) for i in range(members)]
        total += lax.ppermute(parts[distance], "zl", route).astype(jnp.float32)
    return total.astype(jnp.bfloat16)


def solution(mesh):
    split = Mesh(mesh.devices.reshape(2, 4, 8, 4, 2), SEQ + HEAD)
    return jax.shard_map(
        shards,
        mesh=split,
        in_specs=(
            P(SEQ, HEAD, None),
            P(SEQ, HEAD, None),
            P(SEQ, HEAD, None),
            P(HEAD),
            P(HEAD),
            P(HEAD),
            P(HEAD, None),
        ),
        out_specs=P(SEQ + HEAD, None),
        check_vma=False,
    )
```

profile of v0, /device:TPU:23, one launch (start us, length us, event | category | flops | bytes accessed | tf_op | source)
XLA Modules:
  0.0 82.6 jit_solution(2778694369093438343)
XLA Ops:
  0.0 0.9 %pad_maximum_fusion.2.own_ref = bf16[2,192,128]{2,1,0:T(8,128)(2,1)S(1)} fusion(bf16[1,192,128]{2,1,0:T(8,128)(2,1)} %bitcast.23, bf16[1,192,128]{2,1,0:T(8,128)(2,1)} %bitcast.26), kind=kLoop, calls=%fused_computation.11 | loop fusion | flops 49152 | bytes 196608 | tf_op jit(solution)/shard_map/stack | solution.py:161
  0.9 10.6 %collective-permute-start.1 = (bf16[2,192,128]{2,1,0:T(8,128)(2,1)S(1)}, bf16[2,192,128]{2,1,0:T(8,128)(2,1)S(1)}, u32[]{:S(2)}, u32[]{:S(2)}) collective-permute-start(bf16[2,192,128]{2,1,0:T(8,128)(2,1)S(1)} %pad_maximum_fusion.2.own_ref), channel_id=1, source_target_pairs={{0,64},{8,72},{16,80},{24,88},{32,96},{40,104},{48,112},{56,120},{... | collective-permute-start | bytes 294920 | tf_op jit(solution)/shard_map/ppermute | solution.py:162
  11.5 0.7 fusion.4
  12.2 0.6 collective-permute-start
  12.8 0.2 collective-permute-done.1.before_ref
  13.1 1.1 %pack.1 = bf16[8,2,192,128]{3,2,1,0:T(8,128)(2,1)} custom-call(s32[8,128]{1,0:T(8,128)S(1)} %broadcast_in_dim.20.y_ref, bf16[2,192,128]{2,1,0:T(8,128)(2,1)S(1)} %pad_maximum_fusion.2.own_ref, bf16[2,192,128]{2,1,0:T(8,128)(2,1)S(1)} %collective-permute-done.1.before_ref), custom_call_target="tpu_custom_call" | custom-call | tf_op jit(solution)/shard_map/pack/pallas_call | solution.py:43
  14.2 0.7 collective-permute-start.2
  14.9 0.7 collective-permute-start.3
  15.6 0.7 collective-permute-start.4
  16.3 10.6 %all-to-all-start = ((bf16[8,2,192,128]{3,2,1,0:T(8,128)(2,1)}), bf16[8,2,192,128]{3,2,1,0:T(8,128)(2,1)S(1)}, u32[]{:S(2)}, u32[]{:S(2)}) async-start(bf16[8,2,192,128]{3,2,1,0:T(8,128)(2,1)} %pack.1), calls=%async_computation | async-start | bytes 1572864 | tf_op jit(solution)/shard_map/all_to_all | solution.py:166
  26.9 1.3 %collective-permute-start.5 = (bf16[2,4,128]{2,1,0:T(4,128)(2,1)S(1)}, bf16[2,4,128]{2,1,0:T(4,128)(2,1)S(1)}, u32[]{:S(2)}, u32[]{:S(2)}) collective-permute-start(bf16[2,4,128]{2,1,0:T(4,128)(2,1)S(1)} %add.52), channel_id=1, source_target_pairs={{0,56},{8,16},{1,57},{9,17},{2,58},{10,18},{3,59},{11,19},{4,60},{... | collective-permute-start | bytes 6152 | tf_op jit(solution)/shard_map/ppermute | solution.py:174
  28.2 0.7 broadcast_multiply_fusion
  28.9 0.7 concatenate.6
  29.6 5.2 %collective-permute-done.5 = bf16[2,4,128]{2,1,0:T(4,128)(2,1)S(1)} collective-permute-done((bf16[2,4,128]{2,1,0:T(4,128)(2,1)S(1)}, bf16[2,4,128]{2,1,0:T(4,128)(2,1)S(1)}, u32[]{:S(2)}, u32[]{:S(2)}) %collective-permute-start.5) | collective-permute-done | bytes 2080 | tf_op jit(solution)/shard_map/ppermute | solution.py:174
  34.9 1.3 %collective-permute-start.6 = (bf16[2,4,128]{2,1,0:T(4,128)(2,1)S(1)}, bf16[2,4,128]{2,1,0:T(4,128)(2,1)S(1)}, u32[]{:S(2)}, u32[]{:S(2)}) collective-permute-start(bf16[2,4,128]{2,1,0:T(4,128)(2,1)S(1)} %add.53), channel_id=1, source_target_pairs={{56,40},{0,48},{8,24},{16,32},{57,41},{1,49},{9,25},{17,33},{58,42... | collective-permute-start | bytes 6152 | tf_op jit(solution)/shard_map/ppermute | solution.py:174
  36.2 1.0 %fusion.6 = (bf16[2,1,2,24,4,128]{5,4,3,2,1,0:T(4,128)(2,1)S(1)}, bf16[2,1,2,24,4,128]{5,4,3,2,1,0:T(4,128)(2,1)S(1)}) fusion(bf16[2,2,2,24,4,128]{5,4,3,2,1,0:T(4,128)(2,1)} %bitcast.18), kind=kLoop, calls=%fused_computation.17 | loop fusion | bytes 393216 | tf_op jit(solution)/shard_map/slice | solution.py:182
  37.2 1.1 %pad_maximum_fusion = (bf16[2,2,2,24,4,128]{5,4,3,2,1,0:T(4,128)(2,1)S(1)}, bf16[2,2,2,24,4,128]{5,4,3,2,1,0:T(4,128)(2,1)S(1)}) fusion(bf16[2,1,2,24,4,128]{5,4,3,2,1,0:T(4,128)(2,1)S(1)} %get-tuple-element.32, bf16[2,1,2,24,4,128]{5,4,3,2,1,0:T(4,128)(2,1)S(1)} %get-tuple-element.31, bf16[2,2,2,24,4,128]{5,4,3,2,1,0:T(4,128)(2,1)} %bitcast.19, pred[]{:T(512)S(6)} %eq.13), kind=kLoop, calls=%fused_computation.4 | loop fusion | flops 196608 | bytes 786433 | tf_op jit(solution)/shard_map/stack | solution.py:182
  38.4 0.1 fusion.5
  38.5 0.1 pad_maximum_fusion.1
  38.8 4.3 %all-to-all-done.halo_ref = bf16[8,2,192,128]{3,2,1,0:T(8,128)(2,1)S(1)} async-done(((bf16[8,2,192,128]{3,2,1,0:T(8,128)(2,1)}), bf16[8,2,192,128]{3,2,1,0:T(8,128)(2,1)S(1)}, u32[]{:S(2)}, u32[]{:S(2)}) %all-to-all-start) | async-done | bytes 786464 | tf_op jit(solution)/shard_map/all_to_all | solution.py:166
  43.1 0.1 broadcast_in_dim.21.table
  43.2 2.0 %attend.3 = bf16[96,512]{1,0:T(8,128)(2,1)S(1)} custom-call(s32[16,128]{1,0:T(8,128)S(1)} %broadcast_in_dim.21.table, f32[8,128]{1,0:T(8,128)S(1)} %broadcast_in_dim.22.bias, bf16[2,4,96,128]{3,2,1,0:T(8,128)(2,1)S(1)} %bitcast.16, bf16[8,2,192,128]{3,2,1,0:T(8,128)(2,1)S(1)} %all-to-all-done.halo_ref, bf16[2,256,128]{2,1,0:T(8,128)(2,1)S(1)} %fusion.2.near_ref), custom_call_target="tpu_custom_call" | custom-call | flops 2818572288 | bytes 786432 | tf_op jit(solution)/shard_map/attend/pallas_call | solution.py:107
  45.2 0.1 copy-done
  45.4 0.8 convolution_convert_fusion
  46.2 9.4 %collective-permute-start.7 = (bf16[96,4096]{1,0:T(8,128)(2,1)S(1)}, bf16[96,4096]{1,0:T(8,128)(2,1)S(1)}, u32[]{:S(2)}, u32[]{:S(2)}) collective-permute-start(bf16[96,4096]{1,0:T(8,128)(2,1)S(1)} %convolution_convert_fusion), channel_id=1, source_target_pairs={{0,1},{1,0},{2,3},{3,2},{4,5},{5,4},{6,7},{7,6},{8,9},{9,8},{10,11... | collective-permute-start | bytes 2359304 | tf_op jit(solution)/shard_map/ppermute | solution.py:194
  55.6 2.0 %attend.2.rows_ref = bf16[96,512]{1,0:T(8,128)(2,1)S(1)} custom-call(s32[16,128]{1,0:T(8,128)S(1)} %broadcast_in_dim.21.table, f32[8,128]{1,0:T(8,128)S(1)} %broadcast_in_dim.22.bias, bf16[2,4,96,128]{3,2,1,0:T(8,128)(2,1)S(1)} %bitcast.17, bf16[8,2,192,128]{3,2,1,0:T(8,128)(2,1)S(1)} %all-to-all-done.halo_ref, bf16[2,256,128]{2,1,0:T(8,128)(2,1)S(1)} %fusion.2.near_ref), custom_call_target="tpu_custom_call" | custom-call | flops 2818572288 | bytes 786432 | tf_op jit(solution)/shard_map/attend/pallas_call | solution.py:107
  57.7 0.9 %project.1 = (bf16[24,4096]{1,0:T(8,128)(2,1)S(1)}, bf16[24,4096]{1,0:T(8,128)(2,1)S(1)}, bf16[24,4096]{1,0:T(8,128)(2,1)S(1)}, bf16[24,4096]{1,0:T(8,128)(2,1)S(1)}) custom-call(bf16[96,512]{1,0:T(8,128)(2,1)S(1)} %attend.2.rows_ref, bf16[512,4096]{1,0:T(8,128)(2,1)S(1)} %copy-done, bf16[96,4096]{1,0:T(8,128)(2,1)S(1)} %collective-permute-done.7.theirs_ref), custom_call_target="tpu_custom_call" | custom-call | flops 402653184 | bytes 4194304 | tf_op jit(solution)/shard_map/project/pallas_call | solution.py:142
  58.6 4.0 %collective-permute-start.8 = (bf16[24,4096]{1,0:T(8,128)(2,1)S(1)}, bf16[24,4096]{1,0:T(8,128)(2,1)S(1)}, u32[]{:S(2)}, u32[]{:S(2)}) collective-permute-start(bf16[24,4096]{1,0:T(8,128)(2,1)S(1)} %get-tuple-element.24), channel_id=1, source_target_pairs={{0,6},{2,4},{4,2},{6,0},{1,7},{3,5},{5,3},{7,1},{8,14},{10,12},{12... | collective-permute-start | bytes 589832 | tf_op jit(solution)/shard_map/ppermute | solution.py:200
  62.6 4.4 %collective-permute-start.9 = (bf16[24,4096]{1,0:T(8,128)(2,1)S(1)}, bf16[24,4096]{1,0:T(8,128)(2,1)S(1)}, u32[]{:S(2)}, u32[]{:S(2)}) collective-permute-start(bf16[24,4096]{1,0:T(8,128)(2,1)S(1)} %get-tuple-element.25), channel_id=1, source_target_pairs={{0,4},{2,6},{4,0},{6,2},{1,5},{3,7},{5,1},{7,3},{8,12},{10,14},{12... | collective-permute-start | bytes 589832 | tf_op jit(solution)/shard_map/ppermute | solution.py:200
  67.0 2.2 %collective-permute-start.10 = (bf16[24,4096]{1,0:T(8,128)(2,1)S(1)}, bf16[24,4096]{1,0:T(8,128)(2,1)S(1)}, u32[]{:S(2)}, u32[]{:S(2)}) collective-permute-start(bf16[24,4096]{1,0:T(8,128)(2,1)S(1)} %get-tuple-element.26), channel_id=1, source_target_pairs={{0,2},{2,0},{4,6},{6,4},{1,3},{3,1},{5,7},{7,5},{8,10},{10,8},{12,... | collective-permute-start | bytes 589832 | tf_op jit(solution)/shard_map/ppermute | solution.py:200
  69.2 12.6 %collective-permute-done.9 = bf16[24,4096]{1,0:T(8,128)(2,1)S(1)} collective-permute-done((bf16[24,4096]{1,0:T(8,128)(2,1)S(1)}, bf16[24,4096]{1,0:T(8,128)(2,1)S(1)}, u32[]{:S(2)}, u32[]{:S(2)}) %collective-permute-start.9) | collective-permute-done | bytes 196640 | tf_op jit(solution)/shard_map/ppermute | solution.py:200
  81.8 0.8 add_convert_fusion
  (29 shorter events, 0.3 us)
Async XLA Ops:
  0.0 38.7 %copy-start.2 = (bf16[192,1,128]{2,0,1:T(8,128)(2,1)S(1)}, bf16[192,1,128]{2,0,1:T(8,128)(2,1)}, u32[]{:S(2)}) copy-start(bf16[192,1,128]{2,0,1:T(8,128)(2,1)} %param.9) | copy-start | bytes 147460
  0.0 38.7 %copy-start.3 = (bf16[192,1,128]{2,0,1:T(8,128)(2,1)S(1)}, bf16[192,1,128]{2,0,1:T(8,128)(2,1)}, u32[]{:S(2)}) copy-start(bf16[192,1,128]{2,0,1:T(8,128)(2,1)} %param.8) | copy-start | bytes 147460
  0.0 38.6 %copy-start.1 = (bf16[192,4,128]{2,1,0:T(4,128)(2,1)S(1)}, bf16[192,4,128]{2,1,0:T(4,128)(2,1)}, u32[]{:S(2)}) copy-start(bf16[192,4,128]{2,1,0:T(4,128)(2,1)} %param.7) | copy-start | bytes 589828
  0.9 12.2 %collective-permute-start.1 = (bf16[2,192,128]{2,1,0:T(8,128)(2,1)S(1)}, bf16[2,192,128]{2,1,0:T(8,128)(2,1)S(1)}, u32[]{:S(2)}, u32[]{:S(2)}) collective-permute-start(bf16[2,192,128]{2,1,0:T(8,128)(2,1)S(1)} %pad_maximum_fusion.2.own_ref), channel_id=1, source_target_pairs={{0,64},{8,72},{16,80},{24,88},{32,96},{40,104},{48,112},{56,120},{... | collective-permute-start | bytes 294920 | tf_op jit(solution)/shard_map/ppermute | solution.py:162
  12.2 2.0 %collective-permute-start = (bf16[2,4,128]{2,1,0:T(4,128)(2,1)S(1)}, bf16[2,4,128]{2,1,0:T(4,128)(2,1)S(1)}, u32[]{:S(2)}, u32[]{:S(2)}) collective-permute-start(bf16[2,4,128]{2,1,0:T(4,128)(2,1)S(1)} %fusion.4), channel_id=1, source_target_pairs={{0,256},{1,257},{2,258},{3,259},{4,260},{5,261},{6,262},{7,263}} | collective-permute-start | bytes 6152 | tf_op jit(solution)/shard_map/ppermute | solution.py:164
  14.2 0.7 collective-permute-start.2
  14.9 0.7 collective-permute-start.3
  15.6 11.3 %collective-permute-start.4 = (bf16[2,4,128]{2,1,0:T(4,128)(2,1)S(1)}, bf16[2,4,128]{2,1,0:T(4,128)(2,1)S(1)}, u32[]{:S(2)}, u32[]{:S(2)}) collective-permute-start(bf16[2,4,128]{2,1,0:T(4,128)(2,1)S(1)} %add.51), channel_id=1, source_target_pairs={{0,8},{1,9},{2,10},{3,11},{4,12},{5,13},{6,14},{7,15},{64,72},{65,... | collective-permute-start | bytes 6152 | tf_op jit(solution)/shard_map/ppermute | solution.py:174
  16.3 26.8 %all-to-all-start = ((bf16[8,2,192,128]{3,2,1,0:T(8,128)(2,1)}), bf16[8,2,192,128]{3,2,1,0:T(8,128)(2,1)S(1)}, u32[]{:S(2)}, u32[]{:S(2)}) async-start(bf16[8,2,192,128]{3,2,1,0:T(8,128)(2,1)} %pack.1), calls=%async_computation | async-start | bytes 1572864 | tf_op jit(solution)/shard_map/all_to_all | solution.py:166
  26.9 8.0 %collective-permute-start.5 = (bf16[2,4,128]{2,1,0:T(4,128)(2,1)S(1)}, bf16[2,4,128]{2,1,0:T(4,128)(2,1)S(1)}, u32[]{:S(2)}, u32[]{:S(2)}) collective-permute-start(bf16[2,4,128]{2,1,0:T(4,128)(2,1)S(1)} %add.52), channel_id=1, source_target_pairs={{0,56},{8,16},{1,57},{9,17},{2,58},{10,18},{3,59},{11,19},{4,60},{... | collective-permute-start | bytes 6152 | tf_op jit(solution)/shard_map/ppermute | solution.py:174
  34.9 3.8 %collective-permute-start.6 = (bf16[2,4,128]{2,1,0:T(4,128)(2,1)S(1)}, bf16[2,4,128]{2,1,0:T(4,128)(2,1)S(1)}, u32[]{:S(2)}, u32[]{:S(2)}) collective-permute-start(bf16[2,4,128]{2,1,0:T(4,128)(2,1)S(1)} %add.53), channel_id=1, source_target_pairs={{56,40},{0,48},{8,24},{16,32},{57,41},{1,49},{9,25},{17,33},{58,42... | collective-permute-start | bytes 6152 | tf_op jit(solution)/shard_map/ppermute | solution.py:174
  43.2 2.2 %copy-start = (bf16[512,4096]{1,0:T(8,128)(2,1)S(1)}, bf16[512,4096]{1,0:T(8,128)(2,1)}, u32[]{:S(2)}) copy-start(bf16[512,4096]{1,0:T(8,128)(2,1)} %weight_ref.1) | copy-start | bytes 12582916
  46.2 11.5 %collective-permute-start.7 = (bf16[96,4096]{1,0:T(8,128)(2,1)S(1)}, bf16[96,4096]{1,0:T(8,128)(2,1)S(1)}, u32[]{:S(2)}, u32[]{:S(2)}) collective-permute-start(bf16[96,4096]{1,0:T(8,128)(2,1)S(1)} %convolution_convert_fusion), channel_id=1, source_target_pairs={{0,1},{1,0},{2,3},{3,2},{4,5},{5,4},{6,7},{7,6},{8,9},{9,8},{10,11... | collective-permute-start | bytes 2359304 | tf_op jit(solution)/shard_map/ppermute | solution.py:194
  58.6 10.6 %collective-permute-start.8 = (bf16[24,4096]{1,0:T(8,128)(2,1)S(1)}, bf16[24,4096]{1,0:T(8,128)(2,1)S(1)}, u32[]{:S(2)}, u32[]{:S(2)}) collective-permute-start(bf16[24,4096]{1,0:T(8,128)(2,1)S(1)} %get-tuple-element.24), channel_id=1, source_target_pairs={{0,6},{2,4},{4,2},{6,0},{1,7},{3,5},{5,3},{7,1},{8,14},{10,12},{12... | collective-permute-start | bytes 589832 | tf_op jit(solution)/shard_map/ppermute | solution.py:200
  62.6 19.2 %collective-permute-start.9 = (bf16[24,4096]{1,0:T(8,128)(2,1)S(1)}, bf16[24,4096]{1,0:T(8,128)(2,1)S(1)}, u32[]{:S(2)}, u32[]{:S(2)}) collective-permute-start(bf16[24,4096]{1,0:T(8,128)(2,1)S(1)} %get-tuple-element.25), channel_id=1, source_target_pairs={{0,4},{2,6},{4,0},{6,2},{1,5},{3,7},{5,1},{7,3},{8,12},{10,14},{12... | collective-permute-start | bytes 589832 | tf_op jit(solution)/shard_map/ppermute | solution.py:200
  67.0 14.9 %collective-permute-start.10 = (bf16[24,4096]{1,0:T(8,128)(2,1)S(1)}, bf16[24,4096]{1,0:T(8,128)(2,1)S(1)}, u32[]{:S(2)}, u32[]{:S(2)}) collective-permute-start(bf16[24,4096]{1,0:T(8,128)(2,1)S(1)} %get-tuple-element.26), channel_id=1, source_target_pairs={{0,2},{2,0},{4,6},{6,4},{1,3},{3,1},{5,7},{7,5},{8,10},{10,8},{12,... | collective-permute-start | bytes 589832 | tf_op jit(solution)/shard_map/ppermute | solution.py:200
where the time goes:
time: 83.1 us; the launch traced here: 82.6 us
  starting transfers between devices  46.4 us (56%)
  waiting for transfers between devices  22.4 us (27%)
  Pallas kernels  6.08 us (7%)
  other arithmetic  4.4 us (5%)
  local copies, waits for them, and re-layouts  2.19 us (3%)
    ppermute x3, waiting for transfers between devices, shards(): total += lax.ppermute(parts[distance], 'zl', route).astype(jnp.float32)  12.7 us
    all_to_all x1, starting transfers between devices, shards(): lax.all_to_all(sent, 'y', 0, 0, axis_index_groups=[list(ORDER)], tiled=True)  10.6 us
    ppermute x1, starting transfers between devices, shards(): lax.ppermute(stacked, SEQ, [(i, i + row_len) for i in range(seq_len - row...  10.6 us
    ppermute x3, starting transfers between devices, shards(): total += lax.ppermute(parts[distance], 'zl', route).astype(jnp.float32)  10.5 us
    ppermute x1, starting transfers between devices, shards(): theirs = lax.ppermute(theirs, 'core', [(0, 1), (1, 0)])  9.43 us
    ppermute x5, waiting for transfers between devices, shards(): sinks = sinks + lax.ppermute(sinks, axis, route)  5.25 us
    ppermute x5, starting transfers between devices, shards(): sinks = sinks + lax.ppermute(sinks, axis, route)  4.55 us
    all_to_all x1, waiting for transfers between devices, shards(): lax.all_to_all(sent, 'y', 0, 0, axis_index_groups=[list(ORDER)], tiled=True)  4.29 us
  transfers between devices with their start and end apart: 12, of which 4 were waited for; matrix products, arithmetic and copies ran while one was open for 6% of the time, Pallas kernels for 4%

commit v1 on v0

--- a/solution.py
+++ b/solution.py
@@ -15,12 +15,12 @@
 NEG = -1e30
 LOG2E = 1.4426950408889634
 SPREAD = (
-    (SEQ, [(0, 32)]),
-    (SEQ, [(i, i + 8) for i in (0, 32)]),
-    (SEQ, [(i, i + j) for i in (0, 32) for i, j in ((i, 24), (i + 8, 8))]),
-    ("y", [(0, 1)]),
-    ("y", [(0, 7), (1, 2)]),
-    ("y", [(7, 5), (0, 6), (1, 3), (2, 4)]),
+    (SEQ, [(0, 1)]),
+    (SEQ, [(0, 7), (1, 2)]),
+    (SEQ, [(7, 5), (0, 6), (1, 3), (2, 4)]),
+    (SEQ, [(i, i + 8) for i in range(8)]),
+    (SEQ, [(i + j, i + k) for i in range(8) for j, k in ((0, 24), (8, 16))]),
+    ("zh", [(0, 1)]),
 )
 ORDER = (4, 5, 6, 7, 3, 2, 1, 0)
 ALWAYS, NEVER = 1 << 30, -(1 << 30)
@@ -51,17 +51,20 @@
 
 
 def attend_kernel(
-    table, bias, q_ref, halo_ref, near_ref, out_ref, score_ref, prob_ref, *, tok_rows, number
+    table, bias, q_ref, halo_ref, near_ref, out_ref, score_ref, prob_ref, *, tok_rows, number, half
 ):
     heads, rows, width = q_ref.shape[1:]
+    rows = rows // 2
+    chosen = slice(half * rows, (half + 1) * rows)
     first_pos, y, member, part = (table[k : k + 1, :1] for k in (0, 1, 2, 3 + number))
     unit = LOG2E / width**0.5
     halo_len = halo_ref.shape[0] * tok_rows
     span = score_ref.shape[1]
-    per = rows // 4
+    per = rows // 2
     row = lax.broadcasted_iota(jnp.int32, (rows, 1), 0)
-    turn = sum((row >= per * k).astype(jnp.int32) for k in range(1, 4))
-    query_pos = first_pos + (turn ^ member) * (2 * per) + part * per + row - turn * per
+    turn = (row >= per).astype(jnp.int32)
+    query_pos = first_pos + ((turn + 2 * half) ^ member) * (2 * per)
+    query_pos = query_pos + part * per + row - turn * per
     place = lax.broadcasted_iota(jnp.int32, (1, halo_len), 1)
     block = sum((place >= k * tok_rows).astype(jnp.int32) for k in range(1, len(ORDER)))
     source = listed(block)
@@ -71,7 +74,8 @@
     is_sink = near >= tok_rows
     near_pos = jnp.where(is_sink, near - tok_rows, first_pos + near)
     first = (1 - part).astype(jnp.float32).astype(jnp.bfloat16)
-    q = (q_ref[0] * first + q_ref[1] * (1 - first)).reshape(heads * rows, width)
+    q = q_ref[0, :, chosen] * first + q_ref[1, :, chosen] * (1 - first)
+    q = q.reshape(heads * rows, width)
     transposed = (((1,), (1,)), ((), ()))
     keys = jnp.concatenate([halo_ref[:, 0].reshape(halo_len, width), near_ref[0]], axis=0)
     score_ref[...] = lax.dot_general(q, keys, transposed, preferred_element_type=jnp.float32)
@@ -99,13 +103,14 @@
         out_ref[:, h * width : (h + 1) * width] = block.astype(out_ref.dtype)
 
 
-def attend(number, table, sink_bias, q, halo, near):
+def attend(number, half, table, sink_bias, q, halo, near):
     heads, rows, width = q.shape[1:]
+    rows = rows // 2
     tok_rows = halo.shape[2]
     vmem = pl.BlockSpec(memory_space=pltpu.VMEM)
     span = halo.shape[0] * tok_rows + near.shape[1]
     return pl.pallas_call(
-        functools.partial(attend_kernel, tok_rows=tok_rows, number=number),
+        functools.partial(attend_kernel, tok_rows=tok_rows, number=number, half=half),
         out_shape=jax.ShapeDtypeStruct((rows, heads * width), jnp.bfloat16),
         in_specs=[vmem] * 5,
         out_specs=vmem,
@@ -160,15 +165,25 @@
     first_pos = lax.axis_index(SEQ) * tok_rows
     stacked = jnp.stack([key_rows[:, 0], value_rows[:, 0]])
     before = lax.ppermute(stacked, SEQ, [(i, i + row_len) for i in range(seq_len - row_len)])
-    sinks = jnp.where(lax.axis_index(SEQ) == 0, stacked[:, :SINKS], 0)
-    moved = lax.ppermute(sinks, *SPREAD[0])
+    def along_row():
+        sinks = jnp.where(y == 0, stacked[:, :SINKS], 0)
+        for axis, route in SPREAD[:3]:
+            sinks = lax.optimization_barrier(sinks)
+            sinks = sinks + lax.ppermute(sinks, axis, route)
+        return sinks
+
+    sinks = lax.cond(
+        lax.axis_index(("zh", "x")) == 0,
+        along_row,
+        lambda: jnp.zeros((2, SINKS, width), stacked.dtype),
+    )
+    before, sinks = lax.optimization_barrier((before, sinks))
     sent = pack(y, stacked, before, row_len)
     halo = lax.all_to_all(sent, "y", 0, 0, axis_index_groups=[list(ORDER)], tiled=True)
-    sinks, moved, windows, sink_counts, sink_bias, _ = lax.optimization_barrier(
-        (sinks, moved, windows, sink_counts, sink_bias, sent)
-    )
-    sinks = sinks + moved
-    for number, (axis, route) in enumerate(SPREAD[1:], 1):
+    windows, sink_counts, sink_bias, _ = lax.optimization_barrier(
+        (windows, sink_counts, sink_bias, sent)
+    )
+    for number, (axis, route) in enumerate(SPREAD[3:], 3):
         if number == len(SPREAD) - 1:
             sinks, queries = lax.optimization_barrier((sinks, queries))
         sinks = sinks + lax.ppermute(sinks, axis, route)
@@ -189,15 +204,20 @@
     bias = jnp.pad(sink_bias * width**0.5, (0, 8 - heads))[:, None]
     table = jnp.broadcast_to(table, (16, LANES))
     bias = jnp.broadcast_to(bias, (8, LANES))
-    theirs = attend(0, table, bias, q, halo, near)
-    theirs = jnp.dot(theirs, out_weight, preferred_element_type=jnp.float32).astype(jnp.bfloat16)
-    theirs = lax.ppermute(theirs, "core", [(0, 1), (1, 0)])
-    mine = attend(1, table, bias, q, halo, near)
-    parts = project(mine, out_weight, theirs, members)
-    total = parts[0].astype(jnp.float32)
-    for distance in (3, 2, 1):
-        route = [(i, i ^ distance) for i in range(members)]
-        total += lax.ppermute(parts[distance], "zl", route).astype(jnp.float32)
+    total = 0.0
+    for half, distances in ((1, (3, 2)), (0, (1, 0))):
+        theirs = attend(0, half, table, bias, q, halo, near)
+        theirs = jnp.dot(theirs, out_weight, preferred_element_type=jnp.float32)
+        theirs = theirs.astype(jnp.bfloat16)
+        theirs = lax.ppermute(theirs, "core", [(0, 1), (1, 0)])
+        mine = attend(1, half, table, bias, q, halo, near)
+        parts = project(mine, out_weight, theirs, 2)
+        for distance in distances:
+            part = parts[distance % 2]
+            if distance:
+                route = [(i, i ^ distance) for i in range(members)]
+                part = lax.ppermute(part, "zl", route)
+            total += part.astype(jnp.float32)
     return total.astype(jnp.bfloat16)
 
 

time: 83.1 us -> 84.7 us (1.019)
  the two profiles are of different devices: /device:TPU:23 before, /device:TPU:8 now
where the time goes in v1:
time: 84.7 us; the launch traced here: 84.1 us
  starting transfers between devices  41.8 us (49%)
  waiting for transfers between devices  26.7 us (32%)
  Pallas kernels  6.63 us (8%)
  other arithmetic  3.71 us (4%)
  local copies, waits for them, and re-layouts  3.14 us (4%)
  matrix products  1.73 us (2%)
    ppermute x3, waiting for transfers between devices, shards(): part = lax.ppermute(part, 'zl', route)  15.5 us
    ppermute x3, starting transfers between devices, shards(): part = lax.ppermute(part, 'zl', route)  12.3 us
    all_to_all x1, starting transfers between devices, shards(): lax.all_to_all(sent, 'y', 0, 0, axis_index_groups=[list(ORDER)], tiled=True)  9.59 us
    ppermute x3, starting transfers between devices, shards(): sinks = sinks + lax.ppermute(sinks, axis, route)  8.31 us
    ppermute x3, waiting for transfers between devices, along_row(): sinks = sinks + lax.ppermute(sinks, axis, route)  7.81 us
    ppermute x2, starting transfers between devices, shards(): theirs = lax.ppermute(theirs, 'core', [(0, 1), (1, 0)])  4.32 us
    ppermute x3, starting transfers between devices, along_row(): sinks = sinks + lax.ppermute(sinks, axis, route)  3.85 us
    pallas_call x4, Pallas kernels, attend(): pl.pallas_call(functools.partial(attend_kernel, tok_rows=tok_rows, number...  3.84 us
  transfers between devices with their start and end apart: 13, of which 6 were waited for; matrix products, arithmetic and copies ran while one was open for 6% of the time, Pallas kernels for 7%

profile of v1, /device:TPU:8, one launch (start us, length us, event | category | flops | bytes accessed | tf_op | source)
XLA Modules:
  0.0 84.1 jit_solution(18243714063256985923)
XLA Ops:
  0.0 0.9 %pad_maximum_fusion.2.own_ref = bf16[2,192,128]{2,1,0:T(8,128)(2,1)S(1)} fusion(bf16[1,192,128]{2,1,0:T(8,128)(2,1)} %bitcast.27, bf16[1,192,128]{2,1,0:T(8,128)(2,1)} %bitcast.29), kind=kLoop, calls=%fused_computation.12 | loop fusion | flops 49152 | bytes 196608 | tf_op jit(solution)/shard_map/stack | solution.py:166
  0.9 3.4 %collective-permute-start.3 = (bf16[2,192,128]{2,1,0:T(8,128)(2,1)S(1)}, bf16[2,192,128]{2,1,0:T(8,128)(2,1)S(1)}, u32[]{:S(2)}, u32[]{:S(2)}) collective-permute-start(bf16[2,192,128]{2,1,0:T(8,128)(2,1)S(1)} %pad_maximum_fusion.2.own_ref), channel_id=1, source_target_pairs={{0,64},{8,72},{16,80},{24,88},{32,96},{40,104},{48,112},{56,120},{... | collective-permute-start | bytes 294920 | tf_op jit(solution)/shard_map/ppermute | solution.py:167
  4.3 11.7 %conditional.1 = (bf16[2,4,128]{2,1,0:T(4,128)(2,1)S(1)}) conditional(s32[]{:T(128)} %convert_element_type.30, () %tuple.14, (s32[]{:T(128)}, bf16[2,192,128]{2,1,0:T(8,128)(2,1)S(1)}) %tuple.15), branch_computations={%region_0.0_spmd, %region_1.2_spmd} | conditional | flops 4097 | bytes 47242 | solution.py:175
  4.3 1.3 %collective-permute-start = (bf16[2,4,128]{2,1,0:T(4,128)(2,1)S(1)}, bf16[2,4,128]{2,1,0:T(4,128)(2,1)S(1)}, u32[]{:S(2)}, u32[]{:S(2)}) collective-permute-start(bf16[2,4,128]{2,1,0:T(4,128)(2,1)S(1)} %slice_select_fusion), channel_id=1, source_target_pairs={{0,8},{1,9},{2,10},{3,11},{4,12},{5,13},{6,14},{7,15}} | collective-permute-start | bytes 6152 | tf_op jit(solution)/shard_map/cond/branch_1_fun/ppermute | solution.py:172
  5.6 5.2 %collective-permute-done = bf16[2,4,128]{2,1,0:T(4,128)(2,1)S(1)} collective-permute-done((bf16[2,4,128]{2,1,0:T(4,128)(2,1)S(1)}, bf16[2,4,128]{2,1,0:T(4,128)(2,1)S(1)}, u32[]{:S(2)}, u32[]{:S(2)}) %collective-permute-start) | collective-permute-done | bytes 2080 | tf_op jit(solution)/shard_map/cond/branch_1_fun/ppermute | solution.py:172
  10.9 1.3 %collective-permute-start.1 = (bf16[2,4,128]{2,1,0:T(4,128)(2,1)S(1)}, bf16[2,4,128]{2,1,0:T(4,128)(2,1)S(1)}, u32[]{:S(2)}, u32[]{:S(2)}) collective-permute-start(bf16[2,4,128]{2,1,0:T(4,128)(2,1)S(1)} %add.28), channel_id=1, source_target_pairs={{0,56},{8,16},{1,57},{9,17},{2,58},{10,18},{3,59},{11,19},{4,60},{... | collective-permute-start | bytes 6152 | tf_op jit(solution)/shard_map/cond/branch_1_fun/ppermute | solution.py:172
  12.2 1.3 %collective-permute-done.1 = bf16[2,4,128]{2,1,0:T(4,128)(2,1)S(1)} collective-permute-done((bf16[2,4,128]{2,1,0:T(4,128)(2,1)S(1)}, bf16[2,4,128]{2,1,0:T(4,128)(2,1)S(1)}, u32[]{:S(2)}, u32[]{:S(2)}) %collective-permute-start.1) | collective-permute-done | bytes 2080 | tf_op jit(solution)/shard_map/cond/branch_1_fun/ppermute | solution.py:172
  13.5 1.3 %collective-permute-start.2 = (bf16[2,4,128]{2,1,0:T(4,128)(2,1)S(1)}, bf16[2,4,128]{2,1,0:T(4,128)(2,1)S(1)}, u32[]{:S(2)}, u32[]{:S(2)}) collective-permute-start(bf16[2,4,128]{2,1,0:T(4,128)(2,1)S(1)} %add.29), channel_id=1, source_target_pairs={{56,40},{0,48},{8,24},{16,32},{57,41},{1,49},{9,25},{17,33},{58,42... | collective-permute-start | bytes 6152 | tf_op jit(solution)/shard_map/cond/branch_1_fun/ppermute | solution.py:172
  14.8 1.3 %collective-permute-done.2 = bf16[2,4,128]{2,1,0:T(4,128)(2,1)S(1)} collective-permute-done((bf16[2,4,128]{2,1,0:T(4,128)(2,1)S(1)}, bf16[2,4,128]{2,1,0:T(4,128)(2,1)S(1)}, u32[]{:S(2)}, u32[]{:S(2)}) %collective-permute-start.2) | collective-permute-done | bytes 2080 | tf_op jit(solution)/shard_map/cond/branch_1_fun/ppermute | solution.py:172
  16.1 1.3 %collective-permute-start.4 = (bf16[2,4,128]{2,1,0:T(4,128)(2,1)S(1)}, bf16[2,4,128]{2,1,0:T(4,128)(2,1)S(1)}, u32[]{:S(2)}, u32[]{:S(2)}) collective-permute-start(bf16[2,4,128]{2,1,0:T(4,128)(2,1)S(1)} %get-tuple-element.42), channel_id=1, source_target_pairs={{0,64},{8,72},{16,80},{24,88},{32,96},{40,104},{48,112},{56,120},{... | collective-permute-start | bytes 6152 | tf_op jit(solution)/shard_map/ppermute | solution.py:189
  17.4 1.1 %pack.1 = bf16[8,2,192,128]{3,2,1,0:T(8,128)(2,1)} custom-call(s32[8,128]{1,0:T(8,128)S(1)} %broadcast_in_dim.10.y_ref, bf16[2,192,128]{2,1,0:T(8,128)(2,1)S(1)} %pad_maximum_fusion.2.own_ref, bf16[2,192,128]{2,1,0:T(8,128)(2,1)S(1)} %collective-permute-done.3.before_ref), custom_call_target="tpu_custom_call" | custom-call | tf_op jit(solution)/shard_map/pack/pallas_call | solution.py:43
  18.5 9.6 %all-to-all-start = ((bf16[8,2,192,128]{3,2,1,0:T(8,128)(2,1)}), bf16[8,2,192,128]{3,2,1,0:T(8,128)(2,1)S(1)}, u32[]{:S(2)}, u32[]{:S(2)}) async-start(bf16[8,2,192,128]{3,2,1,0:T(8,128)(2,1)} %pack.1), calls=%async_computation | async-start | bytes 1572864 | tf_op jit(solution)/shard_map/all_to_all | solution.py:182
  28.1 1.3 %collective-permute-start.5 = (bf16[2,4,128]{2,1,0:T(4,128)(2,1)S(1)}, bf16[2,4,128]{2,1,0:T(4,128)(2,1)S(1)}, u32[]{:S(2)}, u32[]{:S(2)}) collective-permute-start(bf16[2,4,128]{2,1,0:T(4,128)(2,1)S(1)} %add.51), channel_id=1, source_target_pairs={{0,192},{64,128},{8,200},{72,136},{16,208},{80,144},{24,216},{88,1... | collective-permute-start | bytes 6152 | tf_op jit(solution)/shard_map/ppermute | solution.py:189
  30.8 5.7 %collective-permute-start.6 = (bf16[2,4,128]{2,1,0:T(4,128)(2,1)S(1)}, bf16[2,4,128]{2,1,0:T(4,128)(2,1)S(1)}, u32[]{:S(2)}, u32[]{:S(2)}) collective-permute-start(bf16[2,4,128]{2,1,0:T(4,128)(2,1)S(1)} %add.52), channel_id=1, source_target_pairs={{0,256},{1,257},{2,258},{3,259},{4,260},{5,261},{6,262},{7,263},{8... | collective-permute-start | bytes 6152 | tf_op jit(solution)/shard_map/ppermute | solution.py:189
  36.6 1.0 %fusion.4 = (bf16[2,1,2,24,4,128]{5,4,3,2,1,0:T(4,128)(2,1)S(1)}, bf16[2,1,2,24,4,128]{5,4,3,2,1,0:T(4,128)(2,1)S(1)}) fusion(bf16[2,2,2,24,4,128]{5,4,3,2,1,0:T(4,128)(2,1)} %bitcast.22), kind=kLoop, calls=%fused_computation.15 | loop fusion | bytes 393216 | tf_op jit(solution)/shard_map/slice | solution.py:197
  37.6 1.1 %pad_maximum_fusion = (bf16[2,2,2,24,4,128]{5,4,3,2,1,0:T(4,128)(2,1)S(1)}, bf16[2,2,2,24,4,128]{5,4,3,2,1,0:T(4,128)(2,1)S(1)}) fusion(bf16[2,1,2,24,4,128]{5,4,3,2,1,0:T(4,128)(2,1)S(1)} %get-tuple-element.41, bf16[2,1,2,24,4,128]{5,4,3,2,1,0:T(4,128)(2,1)S(1)} %get-tuple-element.40, bf16[2,2,2,24,4,128]{5,4,3,2,1,0:T(4,128)(2,1)} %bitcast.23, pred[]{:T(512)S(6)} %eq.16), kind=kLoop, calls=%fused_computation.6 | loop fusion | flops 196608 | bytes 786433 | tf_op jit(solution)/shard_map/stack | solution.py:197
  39.2 3.4 %all-to-all-done.halo_ref = bf16[8,2,192,128]{3,2,1,0:T(8,128)(2,1)S(1)} async-done(((bf16[8,2,192,128]{3,2,1,0:T(8,128)(2,1)}), bf16[8,2,192,128]{3,2,1,0:T(8,128)(2,1)S(1)}, u32[]{:S(2)}, u32[]{:S(2)}) %all-to-all-start) | async-done | bytes 786464 | tf_op jit(solution)/shard_map/all_to_all | solution.py:182
  42.7 1.0 %attend.7 = bf16[48,512]{1,0:T(8,128)(2,1)S(1)} custom-call(s32[16,128]{1,0:T(8,128)S(1)} %broadcast_in_dim.20.table, f32[8,128]{1,0:T(8,128)S(1)} %broadcast_in_dim.21.bias, bf16[2,4,96,128]{3,2,1,0:T(8,128)(2,1)S(1)} %bitcast.18, bf16[8,2,192,128]{3,2,1,0:T(8,128)(2,1)S(1)} %all-to-all-done.halo_ref, bf16[2,256,128]{2,1,0:T(8,128)(2,1)S(1)} %fusion.2.near_ref), custom_call_target="tpu_custom_call" | custom-call | flops 1409286144 | bytes 786432 | tf_op jit(solution)/shard_map/attend/pallas_call | solution.py:112
  43.7 1.1 %copy-done = bf16[512,4096]{1,0:T(8,128)(2,1)S(1)} copy-done((bf16[512,4096]{1,0:T(8,128)(2,1)S(1)}, bf16[512,4096]{1,0:T(8,128)(2,1)}, u32[]{:S(2)}) %copy-start) | copy-done | bytes 4194328
  44.8 0.9 %convolution_convert_fusion = bf16[48,4096]{1,0:T(8,128)(2,1)S(1)} fusion(bf16[48,512]{1,0:T(8,128)(2,1)S(1)} %attend.7, bf16[512,4096]{1,0:T(8,128)(2,1)S(1)} %copy-done), kind=kOutput, calls=%fused_computation.1 | convolution fusion | flops 201523200 | bytes 4636672 | tf_op jit(solution)/shard_map/dot_general | solution.py:210
  45.6 1.9 %collective-permute-start.10 = (bf16[48,4096]{1,0:T(8,128)(2,1)S(1)}, bf16[48,4096]{1,0:T(8,128)(2,1)S(1)}, u32[]{:S(2)}, u32[]{:S(2)}) collective-permute-start(bf16[48,4096]{1,0:T(8,128)(2,1)S(1)} %convolution_convert_fusion), channel_id=1, source_target_pairs={{0,1},{1,0},{2,3},{3,2},{4,5},{5,4},{6,7},{7,6},{8,9},{9,8},{10,11... | collective-permute-start | bytes 1179656 | tf_op jit(solution)/shard_map/ppermute | solution.py:212
  47.6 1.0 %attend.5 = bf16[48,512]{1,0:T(8,128)(2,1)S(1)} custom-call(s32[16,128]{1,0:T(8,128)S(1)} %broadcast_in_dim.20.table, f32[8,128]{1,0:T(8,128)S(1)} %broadcast_in_dim.21.bias, bf16[2,4,96,128]{3,2,1,0:T(8,128)(2,1)S(1)} %bitcast.19, bf16[8,2,192,128]{3,2,1,0:T(8,128)(2,1)S(1)} %all-to-all-done.halo_ref, bf16[2,256,128]{2,1,0:T(8,128)(2,1)S(1)} %fusion.2.near_ref), custom_call_target="tpu_custom_call" | custom-call | flops 1409286144 | bytes 786432 | tf_op jit(solution)/shard_map/attend/pallas_call | solution.py:112
  48.5 0.9 %convolution_convert_fusion.1 = bf16[48,4096]{1,0:T(8,128)(2,1)S(1)} fusion(bf16[48,512]{1,0:T(8,128)(2,1)S(1)} %attend.5, bf16[512,4096]{1,0:T(8,128)(2,1)S(1)} %copy-done), kind=kOutput, calls=%fused_computation.2 | convolution fusion | flops 201523200 | bytes 4636672 | tf_op jit(solution)/shard_map/dot_general | solution.py:210
  49.4 2.4 %collective-permute-start.7 = (bf16[48,4096]{1,0:T(8,128)(2,1)S(1)}, bf16[48,4096]{1,0:T(8,128)(2,1)S(1)}, u32[]{:S(2)}, u32[]{:S(2)}) collective-permute-start(bf16[48,4096]{1,0:T(8,128)(2,1)S(1)} %convolution_convert_fusion.1), channel_id=1, source_target_pairs={{0,1},{1,0},{2,3},{3,2},{4,5},{5,4},{6,7},{7,6},{8,9},{9,8},{10,11... | collective-permute-start | bytes 1179656 | tf_op jit(solution)/shard_map/ppermute | solution.py:212
  51.8 1.0 %attend.6.rows_ref = bf16[48,512]{1,0:T(8,128)(2,1)S(1)} custom-call(s32[16,128]{1,0:T(8,128)S(1)} %broadcast_in_dim.20.table, f32[8,128]{1,0:T(8,128)S(1)} %broadcast_in_dim.21.bias, bf16[2,4,96,128]{3,2,1,0:T(8,128)(2,1)S(1)} %bitcast.20, bf16[8,2,192,128]{3,2,1,0:T(8,128)(2,1)S(1)} %all-to-all-done.halo_ref, bf16[2,256,128]{2,1,0:T(8,128)(2,1)S(1)} %fusion.2.near_ref), custom_call_target="tpu_custom_call" | custom-call | flops 1409286144 | bytes 786432 | tf_op jit(solution)/shard_map/attend/pallas_call | solution.py:112
  52.8 1.0 %attend.4.rows_ref = bf16[48,512]{1,0:T(8,128)(2,1)S(1)} custom-call(s32[16,128]{1,0:T(8,128)S(1)} %broadcast_in_dim.20.table, f32[8,128]{1,0:T(8,128)S(1)} %broadcast_in_dim.21.bias, bf16[2,4,96,128]{3,2,1,0:T(8,128)(2,1)S(1)} %bitcast.21, bf16[8,2,192,128]{3,2,1,0:T(8,128)(2,1)S(1)} %all-to-all-done.halo_ref, bf16[2,256,128]{2,1,0:T(8,128)(2,1)S(1)} %fusion.2.near_ref), custom_call_target="tpu_custom_call" | custom-call | flops 1409286144 | bytes 786432 | tf_op jit(solution)/shard_map/attend/pallas_call | solution.py:112
  53.7 0.8 %project.3 = (bf16[24,4096]{1,0:T(8,128)(2,1)S(1)}, bf16[24,4096]{1,0:T(8,128)(2,1)S(1)}) custom-call(bf16[48,512]{1,0:T(8,128)(2,1)S(1)} %attend.6.rows_ref, bf16[512,4096]{1,0:T(8,128)(2,1)S(1)} %copy-done, bf16[48,4096]{1,0:T(8,128)(2,1)S(1)} %collective-permute-done.10.theirs_ref), custom_call_target="tpu_custom_call" | custom-call | flops 201326592 | bytes 4194304 | tf_op jit(solution)/shard_map/project/pallas_call | solution.py:147
  54.6 4.3 %collective-permute-start.11 = (bf16[24,4096]{1,0:T(8,128)(2,1)S(1)}, bf16[24,4096]{1,0:T(8,128)(2,1)S(1)}, u32[]{:S(2)}, u32[]{:S(2)}) collective-permute-start(bf16[24,4096]{1,0:T(8,128)(2,1)S(1)} %get-tuple-element.34), channel_id=1, source_target_pairs={{0,2},{2,0},{4,6},{6,4},{1,3},{3,1},{5,7},{7,5},{8,10},{10,8},{12,... | collective-permute-start | bytes 589832 | tf_op jit(solution)/shard_map/ppermute | solution.py:219
  59.8 5.5 %collective-permute-start.8 = (bf16[24,4096]{1,0:T(8,128)(2,1)S(1)}, bf16[24,4096]{1,0:T(8,128)(2,1)S(1)}, u32[]{:S(2)}, u32[]{:S(2)}) collective-permute-start(bf16[24,4096]{1,0:T(8,128)(2,1)S(1)} %get-tuple-element.32), channel_id=1, source_target_pairs={{0,6},{2,4},{4,2},{6,0},{1,7},{3,5},{5,3},{7,1},{8,14},{10,12},{12... | collective-permute-start | bytes 589832 | tf_op jit(solution)/shard_map/ppermute | solution.py:219
  65.3 2.5 %collective-permute-start.9 = (bf16[24,4096]{1,0:T(8,128)(2,1)S(1)}, bf16[24,4096]{1,0:T(8,128)(2,1)S(1)}, u32[]{:S(2)}, u32[]{:S(2)}) collective-permute-start(bf16[24,4096]{1,0:T(8,128)(2,1)S(1)} %get-tuple-element.33), channel_id=1, source_target_pairs={{0,4},{2,6},{4,0},{6,2},{1,5},{3,7},{5,1},{7,3},{8,12},{10,14},{12... | collective-permute-start | bytes 589832 | tf_op jit(solution)/shard_map/ppermute | solution.py:219
  67.8 4.8 %collective-permute-done.8 = bf16[24,4096]{1,0:T(8,128)(2,1)S(1)} collective-permute-done((bf16[24,4096]{1,0:T(8,128)(2,1)S(1)}, bf16[24,4096]{1,0:T(8,128)(2,1)S(1)}, u32[]{:S(2)}, u32[]{:S(2)}) %collective-permute-start.8) | collective-permute-done | bytes 196640 | tf_op jit(solution)/shard_map/ppermute | solution.py:219
  72.6 10.7 %collective-permute-done.9 = bf16[24,4096]{1,0:T(8,128)(2,1)S(1)} collective-permute-done((bf16[24,4096]{1,0:T(8,128)(2,1)S(1)}, bf16[24,4096]{1,0:T(8,128)(2,1)S(1)}, u32[]{:S(2)}, u32[]{:S(2)}) %collective-permute-start.9) | collective-permute-done | bytes 196640 | tf_op jit(solution)/shard_map/ppermute | solution.py:219
  (36 shorter events, 3.6 us)
Async XLA Ops:
  0.0 39.1 %copy-start.2 = (bf16[192,1,128]{2,0,1:T(8,128)(2,1)S(1)}, bf16[192,1,128]{2,0,1:T(8,128)(2,1)}, u32[]{:S(2)}) copy-start(bf16[192,1,128]{2,0,1:T(8,128)(2,1)} %param.11) | copy-start | bytes 147460
  0.0 39.1 %copy-start.3 = (bf16[192,1,128]{2,0,1:T(8,128)(2,1)S(1)}, bf16[192,1,128]{2,0,1:T(8,128)(2,1)}, u32[]{:S(2)}) copy-start(bf16[192,1,128]{2,0,1:T(8,128)(2,1)} %param.10) | copy-start | bytes 147460
  0.0 39.0 %copy-start.1 = (bf16[192,4,128]{2,1,0:T(4,128)(2,1)S(1)}, bf16[192,4,128]{2,1,0:T(4,128)(2,1)}, u32[]{:S(2)}) copy-start(bf16[192,4,128]{2,1,0:T(4,128)(2,1)} %param.9) | copy-start | bytes 589828
  0.9 15.2 %collective-permute-start.3 = (bf16[2,192,128]{2,1,0:T(8,128)(2,1)S(1)}, bf16[2,192,128]{2,1,0:T(8,128)(2,1)S(1)}, u32[]{:S(2)}, u32[]{:S(2)}) collective-permute-start(bf16[2,192,128]{2,1,0:T(8,128)(2,1)S(1)} %pad_maximum_fusion.2.own_ref), channel_id=1, source_target_pairs={{0,64},{8,72},{16,80},{24,88},{32,96},{40,104},{48,112},{56,120},{... | collective-permute-start | bytes 294920 | tf_op jit(solution)/shard_map/ppermute | solution.py:167
  4.3 6.5 %collective-permute-start = (bf16[2,4,128]{2,1,0:T(4,128)(2,1)S(1)}, bf16[2,4,128]{2,1,0:T(4,128)(2,1)S(1)}, u32[]{:S(2)}, u32[]{:S(2)}) collective-permute-start(bf16[2,4,128]{2,1,0:T(4,128)(2,1)S(1)} %slice_select_fusion), channel_id=1, source_target_pairs={{0,8},{1,9},{2,10},{3,11},{4,12},{5,13},{6,14},{7,15}} | collective-permute-start | bytes 6152 | tf_op jit(solution)/shard_map/cond/branch_1_fun/ppermute | solution.py:172
  10.9 2.6 %collective-permute-start.1 = (bf16[2,4,128]{2,1,0:T(4,128)(2,1)S(1)}, bf16[2,4,128]{2,1,0:T(4,128)(2,1)S(1)}, u32[]{:S(2)}, u32[]{:S(2)}) collective-permute-start(bf16[2,4,128]{2,1,0:T(4,128)(2,1)S(1)} %add.28), channel_id=1, source_target_pairs={{0,56},{8,16},{1,57},{9,17},{2,58},{10,18},{3,59},{11,19},{4,60},{... | collective-permute-start | bytes 6152 | tf_op jit(solution)/shard_map/cond/branch_1_fun/ppermute | solution.py:172
  13.5 2.6 %collective-permute-start.2 = (bf16[2,4,128]{2,1,0:T(4,128)(2,1)S(1)}, bf16[2,4,128]{2,1,0:T(4,128)(2,1)S(1)}, u32[]{:S(2)}, u32[]{:S(2)}) collective-permute-start(bf16[2,4,128]{2,1,0:T(4,128)(2,1)S(1)} %add.29), channel_id=1, source_target_pairs={{56,40},{0,48},{8,24},{16,32},{57,41},{1,49},{9,25},{17,33},{58,42... | collective-permute-start | bytes 6152 | tf_op jit(solution)/shard_map/cond/branch_1_fun/ppermute | solution.py:172
  16.1 12.0 %collective-permute-start.4 = (bf16[2,4,128]{2,1,0:T(4,128)(2,1)S(1)}, bf16[2,4,128]{2,1,0:T(4,128)(2,1)S(1)}, u32[]{:S(2)}, u32[]{:S(2)}) collective-permute-start(bf16[2,4,128]{2,1,0:T(4,128)(2,1)S(1)} %get-tuple-element.42), channel_id=1, source_target_pairs={{0,64},{8,72},{16,80},{24,88},{32,96},{40,104},{48,112},{56,120},{... | collective-permute-start | bytes 6152 | tf_op jit(solution)/shard_map/ppermute | solution.py:189
  18.5 24.1 %all-to-all-start = ((bf16[8,2,192,128]{3,2,1,0:T(8,128)(2,1)}), bf16[8,2,192,128]{3,2,1,0:T(8,128)(2,1)S(1)}, u32[]{:S(2)}, u32[]{:S(2)}) async-start(bf16[8,2,192,128]{3,2,1,0:T(8,128)(2,1)} %pack.1), calls=%async_computation | async-start | bytes 1572864 | tf_op jit(solution)/shard_map/all_to_all | solution.py:182
  28.1 2.7 %collective-permute-start.5 = (bf16[2,4,128]{2,1,0:T(4,128)(2,1)S(1)}, bf16[2,4,128]{2,1,0:T(4,128)(2,1)S(1)}, u32[]{:S(2)}, u32[]{:S(2)}) collective-permute-start(bf16[2,4,128]{2,1,0:T(4,128)(2,1)S(1)} %add.51), channel_id=1, source_target_pairs={{0,192},{64,128},{8,200},{72,136},{16,208},{80,144},{24,216},{88,1... | collective-permute-start | bytes 6152 | tf_op jit(solution)/shard_map/ppermute | solution.py:189
  30.8 8.3 %collective-permute-start.6 = (bf16[2,4,128]{2,1,0:T(4,128)(2,1)S(1)}, bf16[2,4,128]{2,1,0:T(4,128)(2,1)S(1)}, u32[]{:S(2)}, u32[]{:S(2)}) collective-permute-start(bf16[2,4,128]{2,1,0:T(4,128)(2,1)S(1)} %add.52), channel_id=1, source_target_pairs={{0,256},{1,257},{2,258},{3,259},{4,260},{5,261},{6,262},{7,263},{8... | collective-permute-start | bytes 6152 | tf_op jit(solution)/shard_map/ppermute | solution.py:189
  42.6 2.2 %copy-start = (bf16[512,4096]{1,0:T(8,128)(2,1)S(1)}, bf16[512,4096]{1,0:T(8,128)(2,1)}, u32[]{:S(2)}) copy-start(bf16[512,4096]{1,0:T(8,128)(2,1)} %weight_ref.3) | copy-start | bytes 12582916
  45.6 8.1 %collective-permute-start.10 = (bf16[48,4096]{1,0:T(8,128)(2,1)S(1)}, bf16[48,4096]{1,0:T(8,128)(2,1)S(1)}, u32[]{:S(2)}, u32[]{:S(2)}) collective-permute-start(bf16[48,4096]{1,0:T(8,128)(2,1)S(1)} %convolution_convert_fusion), channel_id=1, source_target_pairs={{0,1},{1,0},{2,3},{3,2},{4,5},{5,4},{6,7},{7,6},{8,9},{9,8},{10,11... | collective-permute-start | bytes 1179656 | tf_op jit(solution)/shard_map/ppermute | solution.py:212
  49.4 9.5 %collective-permute-start.7 = (bf16[48,4096]{1,0:T(8,128)(2,1)S(1)}, bf16[48,4096]{1,0:T(8,128)(2,1)S(1)}, u32[]{:S(2)}, u32[]{:S(2)}) collective-permute-start(bf16[48,4096]{1,0:T(8,128)(2,1)S(1)} %convolution_convert_fusion.1), channel_id=1, source_target_pairs={{0,1},{1,0},{2,3},{3,2},{4,5},{5,4},{6,7},{7,6},{8,9},{9,8},{10,11... | collective-permute-start | bytes 1179656 | tf_op jit(solution)/shard_map/ppermute | solution.py:212
  54.6 13.2 %collective-permute-start.11 = (bf16[24,4096]{1,0:T(8,128)(2,1)S(1)}, bf16[24,4096]{1,0:T(8,128)(2,1)S(1)}, u32[]{:S(2)}, u32[]{:S(2)}) collective-permute-start(bf16[24,4096]{1,0:T(8,128)(2,1)S(1)} %get-tuple-element.34), channel_id=1, source_target_pairs={{0,2},{2,0},{4,6},{6,4},{1,3},{3,1},{5,7},{7,5},{8,10},{10,8},{12,... | collective-permute-start | bytes 589832 | tf_op jit(solution)/shard_map/ppermute | solution.py:219
  59.8 12.8 %collective-permute-start.8 = (bf16[24,4096]{1,0:T(8,128)(2,1)S(1)}, bf16[24,4096]{1,0:T(8,128)(2,1)S(1)}, u32[]{:S(2)}, u32[]{:S(2)}) collective-permute-start(bf16[24,4096]{1,0:T(8,128)(2,1)S(1)} %get-tuple-element.32), channel_id=1, source_target_pairs={{0,6},{2,4},{4,2},{6,0},{1,7},{3,5},{5,3},{7,1},{8,14},{10,12},{12... | collective-permute-start | bytes 589832 | tf_op jit(solution)/shard_map/ppermute | solution.py:219
  65.3 18.0 %collective-permute-start.9 = (bf16[24,4096]{1,0:T(8,128)(2,1)S(1)}, bf16[24,4096]{1,0:T(8,128)(2,1)S(1)}, u32[]{:S(2)}, u32[]{:S(2)}) collective-permute-start(bf16[24,4096]{1,0:T(8,128)(2,1)S(1)} %get-tuple-element.33), channel_id=1, source_target_pairs={{0,4},{2,6},{4,0},{6,2},{1,5},{3,7},{5,1},{7,3},{8,12},{10,14},{12... | collective-permute-start | bytes 589832 | tf_op jit(solution)/shard_map/ppermute | solution.py:219

commit v2 on v0

--- a/solution.py
+++ b/solution.py
@@ -15,12 +15,12 @@
 NEG = -1e30
 LOG2E = 1.4426950408889634
 SPREAD = (
-    (SEQ, [(0, 32)]),
-    (SEQ, [(i, i + 8) for i in (0, 32)]),
-    (SEQ, [(i, i + j) for i in (0, 32) for i, j in ((i, 24), (i + 8, 8))]),
-    ("y", [(0, 1)]),
-    ("y", [(0, 7), (1, 2)]),
-    ("y", [(7, 5), (0, 6), (1, 3), (2, 4)]),
+    (SEQ, [(0, 1)]),
+    (SEQ, [(0, 7), (1, 2)]),
+    (SEQ, [(7, 5), (0, 6), (1, 3), (2, 4)]),
+    (SEQ, [(i, i + 8) for i in range(8)]),
+    (SEQ, [(i + j, i + k) for i in range(8) for j, k in ((0, 24), (8, 16))]),
+    ("zh", [(0, 1)]),
 )
 ORDER = (4, 5, 6, 7, 3, 2, 1, 0)
 ALWAYS, NEVER = 1 << 30, -(1 << 30)
@@ -160,15 +160,25 @@
     first_pos = lax.axis_index(SEQ) * tok_rows
     stacked = jnp.stack([key_rows[:, 0], value_rows[:, 0]])
     before = lax.ppermute(stacked, SEQ, [(i, i + row_len) for i in range(seq_len - row_len)])
-    sinks = jnp.where(lax.axis_index(SEQ) == 0, stacked[:, :SINKS], 0)
-    moved = lax.ppermute(sinks, *SPREAD[0])
+    def along_row():
+        sinks = jnp.where(y == 0, stacked[:, :SINKS], 0)
+        for axis, route in SPREAD[:3]:
+            sinks = lax.optimization_barrier(sinks)
+            sinks = sinks + lax.ppermute(sinks, axis, route)
+        return sinks
+
+    sinks = lax.cond(
+        lax.axis_index(("zh", "x")) == 0,
+        along_row,
+        lambda: jnp.zeros((2, SINKS, width), stacked.dtype),
+    )
+    before, sinks = lax.optimization_barrier((before, sinks))
     sent = pack(y, stacked, before, row_len)
     halo = lax.all_to_all(sent, "y", 0, 0, axis_index_groups=[list(ORDER)], tiled=True)
-    sinks, moved, windows, sink_counts, sink_bias, _ = lax.optimization_barrier(
-        (sinks, moved, windows, sink_counts, sink_bias, sent)
-    )
-    sinks = sinks + moved
-    for number, (axis, route) in enumerate(SPREAD[1:], 1):
+    windows, sink_counts, sink_bias, _ = lax.optimization_barrier(
+        (windows, sink_counts, sink_bias, sent)
+    )
+    for number, (axis, route) in enumerate(SPREAD[3:], 3):
         if number == len(SPREAD) - 1:
             sinks, queries = lax.optimization_barrier((sinks, queries))
         sinks = sinks + lax.ppermute(sinks, axis, route)
@@ -195,7 +205,7 @@
     mine = attend(1, table, bias, q, halo, near)
     parts = project(mine, out_weight, theirs, members)
     total = parts[0].astype(jnp.float32)
-    for distance in (3, 2, 1):
+    for distance in (3, 1, 2):
         route = [(i, i ^ distance) for i in range(members)]
         total += lax.ppermute(parts[distance], "zl", route).astype(jnp.float32)
     return total.astype(jnp.bfloat16)

time: 83.1 us -> 75.1 us (0.904)
  the two profiles are of different devices: /device:TPU:23 before, /device:TPU:15 now
where the time goes in v2:
time: 75.1 us; the launch traced here: 74.6 us
  starting transfers between devices  36.3 us (48%)
  waiting for transfers between devices  25.3 us (34%)
  Pallas kernels  6.09 us (8%)
  other arithmetic  3.67 us (5%)
  local copies, waits for them, and re-layouts  2.19 us (3%)
  matrix products  0.82 us (1%)
    ppermute x3, starting transfers between devices, shards(): total += lax.ppermute(parts[distance], 'zl', route).astype(jnp.float32)  12 us
    ppermute x3, waiting for transfers between devices, shards(): total += lax.ppermute(parts[distance], 'zl', route).astype(jnp.float32)  11.2 us
    ppermute x1, starting transfers between devices, shards(): lax.ppermute(stacked, SEQ, [(i, i + row_len) for i in range(seq_len - row...  10.6 us
    all_to_all x1, waiting for transfers between devices, shards(): lax.all_to_all(sent, 'y', 0, 0, axis_index_groups=[list(ORDER)], tiled=True)  8.76 us
    all_to_all x1, starting transfers between devices, shards(): lax.all_to_all(sent, 'y', 0, 0, axis_index_groups=[list(ORDER)], tiled=True)  8.01 us
    pallas_call x2, Pallas kernels, attend(): pl.pallas_call(functools.partial(attend_kernel, tok_rows=tok_rows, number...  4.09 us
    ppermute x3, waiting for transfers between devices, shards(): sinks = sinks + lax.ppermute(sinks, axis, route)  3.77 us
    ppermute x3, starting transfers between devices, shards(): sinks = sinks + lax.ppermute(sinks, axis, route)  3.23 us
  transfers between devices with their start and end apart: 9, of which 6 were waited for; matrix products, arithmetic and copies ran while one was open for 5% of the time, Pallas kernels for 4%

profile of v2, /device:TPU:15, one launch (start us, length us, event | category | flops | bytes accessed | tf_op | source)
XLA Modules:
  0.0 74.6 jit_solution(7017105503251077392)
XLA Ops:
  0.0 0.9 %pad_maximum_fusion.2.own_ref = bf16[2,192,128]{2,1,0:T(8,128)(2,1)S(1)} fusion(bf16[1,192,128]{2,1,0:T(8,128)(2,1)} %bitcast.23, bf16[1,192,128]{2,1,0:T(8,128)(2,1)} %bitcast.25), kind=kLoop, calls=%fused_computation.11 | loop fusion | flops 49152 | bytes 196608 | tf_op jit(solution)/shard_map/stack | solution.py:161
  0.9 10.6 %collective-permute-start.3 = (bf16[2,192,128]{2,1,0:T(8,128)(2,1)S(1)}, bf16[2,192,128]{2,1,0:T(8,128)(2,1)S(1)}, u32[]{:S(2)}, u32[]{:S(2)}) collective-permute-start(bf16[2,192,128]{2,1,0:T(8,128)(2,1)S(1)} %pad_maximum_fusion.2.own_ref), channel_id=1, source_target_pairs={{0,64},{8,72},{16,80},{24,88},{32,96},{40,104},{48,112},{56,120},{... | collective-permute-start | bytes 294920 | tf_op jit(solution)/shard_map/ppermute | solution.py:162
  11.5 1.6 %collective-permute-done.3.before_ref = bf16[2,192,128]{2,1,0:T(8,128)(2,1)S(1)} collective-permute-done((bf16[2,192,128]{2,1,0:T(8,128)(2,1)S(1)}, bf16[2,192,128]{2,1,0:T(8,128)(2,1)S(1)}, u32[]{:S(2)}, u32[]{:S(2)}) %collective-permute-start.3) | collective-permute-done | bytes 98336 | tf_op jit(solution)/shard_map/ppermute | solution.py:162
  13.1 0.6 collective-permute-start.4
  13.8 1.1 %pack.1 = bf16[8,2,192,128]{3,2,1,0:T(8,128)(2,1)} custom-call(s32[8,128]{1,0:T(8,128)S(1)} %broadcast_in_dim.10.y_ref, bf16[2,192,128]{2,1,0:T(8,128)(2,1)S(1)} %pad_maximum_fusion.2.own_ref, bf16[2,192,128]{2,1,0:T(8,128)(2,1)S(1)} %collective-permute-done.3.before_ref), custom_call_target="tpu_custom_call" | custom-call | tf_op jit(solution)/shard_map/pack/pallas_call | solution.py:43
  14.9 8.0 %all-to-all-start = ((bf16[8,2,192,128]{3,2,1,0:T(8,128)(2,1)}), bf16[8,2,192,128]{3,2,1,0:T(8,128)(2,1)S(1)}, u32[]{:S(2)}, u32[]{:S(2)}) async-start(bf16[8,2,192,128]{3,2,1,0:T(8,128)(2,1)} %pack.1), calls=%async_computation | async-start | bytes 1572864 | tf_op jit(solution)/shard_map/all_to_all | solution.py:177
  22.9 0.0 collective-permute-done.4
  22.9 1.3 %collective-permute-start.5 = (bf16[2,4,128]{2,1,0:T(4,128)(2,1)S(1)}, bf16[2,4,128]{2,1,0:T(4,128)(2,1)S(1)}, u32[]{:S(2)}, u32[]{:S(2)}) collective-permute-start(bf16[2,4,128]{2,1,0:T(4,128)(2,1)S(1)} %add.51), channel_id=1, source_target_pairs={{0,192},{64,128},{8,200},{72,136},{16,208},{80,144},{24,216},{88,1... | collective-permute-start | bytes 6152 | tf_op jit(solution)/shard_map/ppermute | solution.py:184
  24.2 0.7 broadcast_multiply_fusion
  24.9 0.7 %concatenate.6 = s32[13]{0:T(128)S(1)} concatenate(s32[1]{0:T(128)} %bitcast, s32[1]{0:T(128)} %bitcast.1, s32[1]{0:T(128)} %bitcast.2, s32[1]{0:T(128)} %bitcast.3, s32[1]{0:T(128)} %bitcast.4, s32[4]{0:T(128)} %param.12, s32[4]{0:T(128)} %param.13), dimensions={0} | concatenate | bytes 104 | tf_op jit(solution)/shard_map/concatenate | solution.py:197
  25.6 3.1 %collective-permute-done.5 = bf16[2,4,128]{2,1,0:T(4,128)(2,1)S(1)} collective-permute-done((bf16[2,4,128]{2,1,0:T(4,128)(2,1)S(1)}, bf16[2,4,128]{2,1,0:T(4,128)(2,1)S(1)}, u32[]{:S(2)}, u32[]{:S(2)}) %collective-permute-start.5) | collective-permute-done | bytes 2080 | tf_op jit(solution)/shard_map/ppermute | solution.py:184
  28.7 1.0 %fusion.4 = (bf16[2,1,2,24,4,128]{5,4,3,2,1,0:T(4,128)(2,1)S(1)}, bf16[2,1,2,24,4,128]{5,4,3,2,1,0:T(4,128)(2,1)S(1)}) fusion(bf16[2,2,2,24,4,128]{5,4,3,2,1,0:T(4,128)(2,1)} %bitcast.18), kind=kLoop, calls=%fused_computation.14 | loop fusion | bytes 393216 | tf_op jit(solution)/shard_map/slice | solution.py:192
  29.8 1.1 %pad_maximum_fusion = (bf16[2,2,2,24,4,128]{5,4,3,2,1,0:T(4,128)(2,1)S(1)}, bf16[2,2,2,24,4,128]{5,4,3,2,1,0:T(4,128)(2,1)S(1)}) fusion(bf16[2,1,2,24,4,128]{5,4,3,2,1,0:T(4,128)(2,1)S(1)} %get-tuple-element.41, bf16[2,1,2,24,4,128]{5,4,3,2,1,0:T(4,128)(2,1)S(1)} %get-tuple-element.40, bf16[2,2,2,24,4,128]{5,4,3,2,1,0:T(4,128)(2,1)} %bitcast.19, pred[]{:T(512)S(6)} %eq.16), kind=kLoop, calls=%fused_computation.5 | loop fusion | flops 196608 | bytes 786433 | tf_op jit(solution)/shard_map/stack | solution.py:192
  30.9 0.1 fusion.3
  31.0 0.1 pad_maximum_fusion.1
  31.2 1.3 %collective-permute-start.6 = (bf16[2,4,128]{2,1,0:T(4,128)(2,1)S(1)}, bf16[2,4,128]{2,1,0:T(4,128)(2,1)S(1)}, u32[]{:S(2)}, u32[]{:S(2)}) collective-permute-start(bf16[2,4,128]{2,1,0:T(4,128)(2,1)S(1)} %add.52), channel_id=1, source_target_pairs={{0,256},{1,257},{2,258},{3,259},{4,260},{5,261},{6,262},{7,263},{8... | collective-permute-start | bytes 6152 | tf_op jit(solution)/shard_map/ppermute | solution.py:184
  32.6 0.7 collective-permute-done.6
  33.3 8.8 %all-to-all-done.halo_ref = bf16[8,2,192,128]{3,2,1,0:T(8,128)(2,1)S(1)} async-done(((bf16[8,2,192,128]{3,2,1,0:T(8,128)(2,1)}), bf16[8,2,192,128]{3,2,1,0:T(8,128)(2,1)S(1)}, u32[]{:S(2)}, u32[]{:S(2)}) %all-to-all-start) | async-done | bytes 786464 | tf_op jit(solution)/shard_map/all_to_all | solution.py:177
  42.0 0.1 broadcast_in_dim.20.table
  42.1 0.1 broadcast_in_dim.21.bias
  42.2 2.0 %attend.3 = bf16[96,512]{1,0:T(8,128)(2,1)S(1)} custom-call(s32[16,128]{1,0:T(8,128)S(1)} %broadcast_in_dim.20.table, f32[8,128]{1,0:T(8,128)S(1)} %broadcast_in_dim.21.bias, bf16[2,4,96,128]{3,2,1,0:T(8,128)(2,1)S(1)} %bitcast.16, bf16[8,2,192,128]{3,2,1,0:T(8,128)(2,1)S(1)} %all-to-all-done.halo_ref, bf16[2,256,128]{2,1,0:T(8,128)(2,1)S(1)} %fusion.2.near_ref), custom_call_target="tpu_custom_call" | custom-call | flops 2818572288 | bytes 786432 | tf_op jit(solution)/shard_map/attend/pallas_call | solution.py:107
  44.2 0.1 copy-done
  44.3 0.8 %convolution_convert_fusion = bf16[96,4096]{1,0:T(8,128)(2,1)S(1)} fusion(bf16[96,512]{1,0:T(8,128)(2,1)S(1)} %attend.3, bf16[512,4096]{1,0:T(8,128)(2,1)S(1)} %copy-done), kind=kOutput, calls=%fused_computation.1 | convolution fusion | flops 403046400 | bytes 5079040 | tf_op jit(solution)/shard_map/dot_general | solution.py:203
  45.2 2.5 %collective-permute-start.7 = (bf16[96,4096]{1,0:T(8,128)(2,1)S(1)}, bf16[96,4096]{1,0:T(8,128)(2,1)S(1)}, u32[]{:S(2)}, u32[]{:S(2)}) collective-permute-start(bf16[96,4096]{1,0:T(8,128)(2,1)S(1)} %convolution_convert_fusion), channel_id=1, source_target_pairs={{0,1},{1,0},{2,3},{3,2},{4,5},{5,4},{6,7},{7,6},{8,9},{9,8},{10,11... | collective-permute-start | bytes 2359304 | tf_op jit(solution)/shard_map/ppermute | solution.py:204
  47.7 2.0 %attend.2.rows_ref = bf16[96,512]{1,0:T(8,128)(2,1)S(1)} custom-call(s32[16,128]{1,0:T(8,128)S(1)} %broadcast_in_dim.20.table, f32[8,128]{1,0:T(8,128)S(1)} %broadcast_in_dim.21.bias, bf16[2,4,96,128]{3,2,1,0:T(8,128)(2,1)S(1)} %bitcast.17, bf16[8,2,192,128]{3,2,1,0:T(8,128)(2,1)S(1)} %all-to-all-done.halo_ref, bf16[2,256,128]{2,1,0:T(8,128)(2,1)S(1)} %fusion.2.near_ref), custom_call_target="tpu_custom_call" | custom-call | flops 2818572288 | bytes 786432 | tf_op jit(solution)/shard_map/attend/pallas_call | solution.py:107
  49.7 0.9 %project.1 = (bf16[24,4096]{1,0:T(8,128)(2,1)S(1)}, bf16[24,4096]{1,0:T(8,128)(2,1)S(1)}, bf16[24,4096]{1,0:T(8,128)(2,1)S(1)}, bf16[24,4096]{1,0:T(8,128)(2,1)S(1)}) custom-call(bf16[96,512]{1,0:T(8,128)(2,1)S(1)} %attend.2.rows_ref, bf16[512,4096]{1,0:T(8,128)(2,1)S(1)} %copy-done, bf16[96,4096]{1,0:T(8,128)(2,1)S(1)} %collective-permute-done.7.theirs_ref), custom_call_target="tpu_custom_call" | custom-call | flops 402653184 | bytes 4194304 | tf_op jit(solution)/shard_map/project/pallas_call | solution.py:142
  50.6 7.0 %collective-permute-start.10 = (bf16[24,4096]{1,0:T(8,128)(2,1)S(1)}, bf16[24,4096]{1,0:T(8,128)(2,1)S(1)}, u32[]{:S(2)}, u32[]{:S(2)}) collective-permute-start(bf16[24,4096]{1,0:T(8,128)(2,1)S(1)} %get-tuple-element.35), channel_id=1, source_target_pairs={{0,4},{2,6},{4,0},{6,2},{1,5},{3,7},{5,1},{7,3},{8,12},{10,14},{12... | collective-permute-start | bytes 589832 | tf_op jit(solution)/shard_map/ppermute | solution.py:210
  57.6 1.9 %collective-permute-start.9 = (bf16[24,4096]{1,0:T(8,128)(2,1)S(1)}, bf16[24,4096]{1,0:T(8,128)(2,1)S(1)}, u32[]{:S(2)}, u32[]{:S(2)}) collective-permute-start(bf16[24,4096]{1,0:T(8,128)(2,1)S(1)} %get-tuple-element.34), channel_id=1, source_target_pairs={{0,2},{2,0},{4,6},{6,4},{1,3},{3,1},{5,7},{7,5},{8,10},{10,8},{12,... | collective-permute-start | bytes 589832 | tf_op jit(solution)/shard_map/ppermute | solution.py:210
  59.6 3.1 %collective-permute-start.8 = (bf16[24,4096]{1,0:T(8,128)(2,1)S(1)}, bf16[24,4096]{1,0:T(8,128)(2,1)S(1)}, u32[]{:S(2)}, u32[]{:S(2)}) collective-permute-start(bf16[24,4096]{1,0:T(8,128)(2,1)S(1)} %get-tuple-element.33), channel_id=1, source_target_pairs={{0,6},{2,4},{4,2},{6,0},{1,7},{3,5},{5,3},{7,1},{8,14},{10,12},{12... | collective-permute-start | bytes 589832 | tf_op jit(solution)/shard_map/ppermute | solution.py:210
  62.6 2.8 %collective-permute-done.10 = bf16[24,4096]{1,0:T(8,128)(2,1)S(1)} collective-permute-done((bf16[24,4096]{1,0:T(8,128)(2,1)S(1)}, bf16[24,4096]{1,0:T(8,128)(2,1)S(1)}, u32[]{:S(2)}, u32[]{:S(2)}) %collective-permute-start.10) | collective-permute-done | bytes 196640 | tf_op jit(solution)/shard_map/ppermute | solution.py:210
  65.5 8.3 %collective-permute-done.9 = bf16[24,4096]{1,0:T(8,128)(2,1)S(1)} collective-permute-done((bf16[24,4096]{1,0:T(8,128)(2,1)S(1)}, bf16[24,4096]{1,0:T(8,128)(2,1)S(1)}, u32[]{:S(2)}, u32[]{:S(2)}) %collective-permute-start.9) | collective-permute-done | bytes 196640 | tf_op jit(solution)/shard_map/ppermute | solution.py:210
  73.8 0.8 %add_convert_fusion = bf16[24,4096]{1,0:T(8,128)(2,1)} fusion(bf16[24,4096]{1,0:T(8,128)(2,1)S(1)} %collective-permute-done.10, bf16[24,4096]{1,0:T(8,128)(2,1)S(1)} %collective-permute-done.9, bf16[24,4096]{1,0:T(8,128)(2,1)S(1)} %collective-permute-done.8, bf16[24,4096]{1,0:T(8,128)(2,1)S(1)} %get-tuple-element.32), kind=kLoop, calls=%fused_computation.2 | loop fusion | flops 786432 | bytes 983040 | tf_op jit(solution)/shard_map/convert_element_type | solution.py:211
  (21 shorter events, 0.2 us)
Async XLA Ops:
  0.0 33.2 %copy-start.2 = (bf16[192,1,128]{2,0,1:T(8,128)(2,1)S(1)}, bf16[192,1,128]{2,0,1:T(8,128)(2,1)}, u32[]{:S(2)}) copy-start(bf16[192,1,128]{2,0,1:T(8,128)(2,1)} %param.11) | copy-start | bytes 147460
  0.0 33.2 %copy-start.3 = (bf16[192,1,128]{2,0,1:T(8,128)(2,1)S(1)}, bf16[192,1,128]{2,0,1:T(8,128)(2,1)}, u32[]{:S(2)}) copy-start(bf16[192,1,128]{2,0,1:T(8,128)(2,1)} %param.10) | copy-start | bytes 147460
  0.0 32.5 %copy-start.1 = (bf16[192,4,128]{2,1,0:T(4,128)(2,1)S(1)}, bf16[192,4,128]{2,1,0:T(4,128)(2,1)}, u32[]{:S(2)}) copy-start(bf16[192,4,128]{2,1,0:T(4,128)(2,1)} %param.9) | copy-start | bytes 589828
  0.9 12.2 %collective-permute-start.3 = (bf16[2,192,128]{2,1,0:T(8,128)(2,1)S(1)}, bf16[2,192,128]{2,1,0:T(8,128)(2,1)S(1)}, u32[]{:S(2)}, u32[]{:S(2)}) collective-permute-start(bf16[2,192,128]{2,1,0:T(8,128)(2,1)S(1)} %pad_maximum_fusion.2.own_ref), channel_id=1, source_target_pairs={{0,64},{8,72},{16,80},{24,88},{32,96},{40,104},{48,112},{56,120},{... | collective-permute-start | bytes 294920 | tf_op jit(solution)/shard_map/ppermute | solution.py:162
  13.1 9.8 %collective-permute-start.4 = (bf16[2,4,128]{2,1,0:T(4,128)(2,1)S(1)}, bf16[2,4,128]{2,1,0:T(4,128)(2,1)S(1)}, u32[]{:S(2)}, u32[]{:S(2)}) collective-permute-start(bf16[2,4,128]{2,1,0:T(4,128)(2,1)S(1)} %get-tuple-element.42), channel_id=1, source_target_pairs={{0,64},{8,72},{16,80},{24,88},{32,96},{40,104},{48,112},{56,120},{... | collective-permute-start | bytes 6152 | tf_op jit(solution)/shard_map/ppermute | solution.py:184
  14.9 27.1 %all-to-all-start = ((bf16[8,2,192,128]{3,2,1,0:T(8,128)(2,1)}), bf16[8,2,192,128]{3,2,1,0:T(8,128)(2,1)S(1)}, u32[]{:S(2)}, u32[]{:S(2)}) async-start(bf16[8,2,192,128]{3,2,1,0:T(8,128)(2,1)} %pack.1), calls=%async_computation | async-start | bytes 1572864 | tf_op jit(solution)/shard_map/all_to_all | solution.py:177
  22.9 5.8 %collective-permute-start.5 = (bf16[2,4,128]{2,1,0:T(4,128)(2,1)S(1)}, bf16[2,4,128]{2,1,0:T(4,128)(2,1)S(1)}, u32[]{:S(2)}, u32[]{:S(2)}) collective-permute-start(bf16[2,4,128]{2,1,0:T(4,128)(2,1)S(1)} %add.51), channel_id=1, source_target_pairs={{0,192},{64,128},{8,200},{72,136},{16,208},{80,144},{24,216},{88,1... | collective-permute-start | bytes 6152 | tf_op jit(solution)/shard_map/ppermute | solution.py:184
  31.2 2.0 %collective-permute-start.6 = (bf16[2,4,128]{2,1,0:T(4,128)(2,1)S(1)}, bf16[2,4,128]{2,1,0:T(4,128)(2,1)S(1)}, u32[]{:S(2)}, u32[]{:S(2)}) collective-permute-start(bf16[2,4,128]{2,1,0:T(4,128)(2,1)S(1)} %add.52), channel_id=1, source_target_pairs={{0,256},{1,257},{2,258},{3,259},{4,260},{5,261},{6,262},{7,263},{8... | collective-permute-start | bytes 6152 | tf_op jit(solution)/shard_map/ppermute | solution.py:184
  42.2 2.2 %copy-start = (bf16[512,4096]{1,0:T(8,128)(2,1)S(1)}, bf16[512,4096]{1,0:T(8,128)(2,1)}, u32[]{:S(2)}) copy-start(bf16[512,4096]{1,0:T(8,128)(2,1)} %weight_ref.1) | copy-start | bytes 12582916
  45.2 4.6 %collective-permute-start.7 = (bf16[96,4096]{1,0:T(8,128)(2,1)S(1)}, bf16[96,4096]{1,0:T(8,128)(2,1)S(1)}, u32[]{:S(2)}, u32[]{:S(2)}) collective-permute-start(bf16[96,4096]{1,0:T(8,128)(2,1)S(1)} %convolution_convert_fusion), channel_id=1, source_target_pairs={{0,1},{1,0},{2,3},{3,2},{4,5},{5,4},{6,7},{7,6},{8,9},{9,8},{10,11... | collective-permute-start | bytes 2359304 | tf_op jit(solution)/shard_map/ppermute | solution.py:204
  50.6 14.9 %collective-permute-start.10 = (bf16[24,4096]{1,0:T(8,128)(2,1)S(1)}, bf16[24,4096]{1,0:T(8,128)(2,1)S(1)}, u32[]{:S(2)}, u32[]{:S(2)}) collective-permute-start(bf16[24,4096]{1,0:T(8,128)(2,1)S(1)} %get-tuple-element.35), channel_id=1, source_target_pairs={{0,4},{2,6},{4,0},{6,2},{1,5},{3,7},{5,1},{7,3},{8,12},{10,14},{12... | collective-permute-start | bytes 589832 | tf_op jit(solution)/shard_map/ppermute | solution.py:210
  57.6 16.2 %collective-permute-start.9 = (bf16[24,4096]{1,0:T(8,128)(2,1)S(1)}, bf16[24,4096]{1,0:T(8,128)(2,1)S(1)}, u32[]{:S(2)}, u32[]{:S(2)}) collective-permute-start(bf16[24,4096]{1,0:T(8,128)(2,1)S(1)} %get-tuple-element.34), channel_id=1, source_target_pairs={{0,2},{2,0},{4,6},{6,4},{1,3},{3,1},{5,7},{7,5},{8,10},{10,8},{12,... | collective-permute-start | bytes 589832 | tf_op jit(solution)/shard_map/ppermute | solution.py:210
  59.6 14.3 %collective-permute-start.8 = (bf16[24,4096]{1,0:T(8,128)(2,1)S(1)}, bf16[24,4096]{1,0:T(8,128)(2,1)S(1)}, u32[]{:S(2)}, u32[]{:S(2)}) collective-permute-start(bf16[24,4096]{1,0:T(8,128)(2,1)S(1)} %get-tuple-element.33), channel_id=1, source_target_pairs={{0,6},{2,4},{4,2},{6,0},{1,7},{3,5},{5,3},{7,1},{8,14},{10,12},{12... | collective-permute-start | bytes 589832 | tf_op jit(solution)/shard_map/ppermute | solution.py:210

commit v3 on v2

--- a/solution.py
+++ b/solution.py
@@ -159,18 +159,23 @@
     y, core = lax.axis_index("y"), lax.axis_index("core")
     first_pos = lax.axis_index(SEQ) * tok_rows
     stacked = jnp.stack([key_rows[:, 0], value_rows[:, 0]])
-    before = lax.ppermute(stacked, SEQ, [(i, i + row_len) for i in range(seq_len - row_len)])
-    def along_row():
-        sinks = jnp.where(y == 0, stacked[:, :SINKS], 0)
-        for axis, route in SPREAD[:3]:
+    first_row = lax.axis_index(("zh", "x")) == 0
+
+    def along_row(steps, sinks):
+        for axis, route in steps:
             sinks = lax.optimization_barrier(sinks)
             sinks = sinks + lax.ppermute(sinks, axis, route)
         return sinks
 
     sinks = lax.cond(
-        lax.axis_index(("zh", "x")) == 0,
-        along_row,
+        first_row,
+        lambda: along_row(SPREAD[:1], jnp.where(y == 0, stacked[:, :SINKS], 0)),
         lambda: jnp.zeros((2, SINKS, width), stacked.dtype),
+    )
+    stacked, sinks = lax.optimization_barrier((stacked, sinks))
+    before = lax.ppermute(stacked, SEQ, [(i, i + row_len) for i in range(seq_len - row_len)])
+    sinks = lax.cond(
+        first_row, lambda v: along_row(SPREAD[1:3], v), lambda v: v, sinks
     )
     before, sinks = lax.optimization_barrier((before, sinks))
     sent = pack(y, stacked, before, row_len)

time: 75.1 us -> 75.1 us (level)
  no operation moved by 1% of the time
where the time goes in v3:
time: 75.1 us; the launch traced here: 74.6 us
  starting transfers between devices  36.3 us (48%)
  waiting for transfers between devices  25.3 us (34%)
  Pallas kernels  6.07 us (8%)
  other arithmetic  3.67 us (5%)
  local copies, waits for them, and re-layouts  2.18 us (3%)
  matrix products  0.83 us (1%)
    ppermute x3, starting transfers between devices, shards(): total += lax.ppermute(parts[distance], 'zl', route).astype(jnp.float32)  12 us
    ppermute x3, waiting for transfers between devices, shards(): total += lax.ppermute(parts[distance], 'zl', route).astype(jnp.float32)  11.2 us
    ppermute x1, starting transfers between devices, shards(): lax.ppermute(stacked, SEQ, [(i, i + row_len) for i in range(seq_len - row...  10.6 us
    all_to_all x1, waiting for transfers between devices, shards(): lax.all_to_all(sent, 'y', 0, 0, axis_index_groups=[list(ORDER)], tiled=True)  8.78 us
    all_to_all x1, starting transfers between devices, shards(): lax.all_to_all(sent, 'y', 0, 0, axis_index_groups=[list(ORDER)], tiled=True)  8.01 us
    pallas_call x2, Pallas kernels, attend(): pl.pallas_call(functools.partial(attend_kernel, tok_rows=tok_rows, number...  4.09 us
    ppermute x3, waiting for transfers between devices, shards(): sinks = sinks + lax.ppermute(sinks, axis, route)  3.77 us
    ppermute x3, starting transfers between devices, shards(): sinks = sinks + lax.ppermute(sinks, axis, route)  3.23 us
  transfers between devices with their start and end apart: 9, of which 6 were waited for; matrix products, arithmetic and copies ran while one was open for 5% of the time, Pallas kernels for 4%

profile of v3, /device:TPU:15, one launch (start us, length us, event | category | flops | bytes accessed | tf_op | source)
XLA Modules:
  0.0 74.6 jit_solution(10298038233169038059)
XLA Ops:
  0.0 0.9 %pad_maximum_fusion.2.own_ref = bf16[2,192,128]{2,1,0:T(8,128)(2,1)S(1)} fusion(bf16[1,192,128]{2,1,0:T(8,128)(2,1)} %bitcast.23, bf16[1,192,128]{2,1,0:T(8,128)(2,1)} %bitcast.24), kind=kLoop, calls=%fused_computation.11 | loop fusion | flops 49152 | bytes 196608 | tf_op jit(solution)/shard_map/stack | solution.py:161
  0.9 10.6 %collective-permute-start.3 = (bf16[2,192,128]{2,1,0:T(8,128)(2,1)S(1)}, bf16[2,192,128]{2,1,0:T(8,128)(2,1)S(1)}, u32[]{:S(2)}, u32[]{:S(2)}) collective-permute-start(bf16[2,192,128]{2,1,0:T(8,128)(2,1)S(1)} %pad_maximum_fusion.2.own_ref), channel_id=1, source_target_pairs={{0,64},{8,72},{16,80},{24,88},{32,96},{40,104},{48,112},{56,120},{... | collective-permute-start | bytes 294920 | tf_op jit(solution)/shard_map/ppermute | solution.py:176
  11.5 1.6 %collective-permute-done.3.before_ref = bf16[2,192,128]{2,1,0:T(8,128)(2,1)S(1)} collective-permute-done((bf16[2,192,128]{2,1,0:T(8,128)(2,1)S(1)}, bf16[2,192,128]{2,1,0:T(8,128)(2,1)S(1)}, u32[]{:S(2)}, u32[]{:S(2)}) %collective-permute-start.3) | collective-permute-done | bytes 98336 | tf_op jit(solution)/shard_map/ppermute | solution.py:176
  13.1 0.6 collective-permute-start.4
  13.8 1.1 %pack.1 = bf16[8,2,192,128]{3,2,1,0:T(8,128)(2,1)} custom-call(s32[8,128]{1,0:T(8,128)S(1)} %broadcast_in_dim.10.y_ref, bf16[2,192,128]{2,1,0:T(8,128)(2,1)S(1)} %pad_maximum_fusion.2.own_ref, bf16[2,192,128]{2,1,0:T(8,128)(2,1)S(1)} %collective-permute-done.3.before_ref), custom_call_target="tpu_custom_call" | custom-call | tf_op jit(solution)/shard_map/pack/pallas_call | solution.py:43
  14.9 8.0 %all-to-all-start = ((bf16[8,2,192,128]{3,2,1,0:T(8,128)(2,1)}), bf16[8,2,192,128]{3,2,1,0:T(8,128)(2,1)S(1)}, u32[]{:S(2)}, u32[]{:S(2)}) async-start(bf16[8,2,192,128]{3,2,1,0:T(8,128)(2,1)} %pack.1), calls=%async_computation | async-start | bytes 1572864 | tf_op jit(solution)/shard_map/all_to_all | solution.py:182
  22.9 0.0 collective-permute-done.4
  22.9 1.3 %collective-permute-start.5 = (bf16[2,4,128]{2,1,0:T(4,128)(2,1)S(1)}, bf16[2,4,128]{2,1,0:T(4,128)(2,1)S(1)}, u32[]{:S(2)}, u32[]{:S(2)}) collective-permute-start(bf16[2,4,128]{2,1,0:T(4,128)(2,1)S(1)} %add.51), channel_id=1, source_target_pairs={{0,192},{64,128},{8,200},{72,136},{16,208},{80,144},{24,216},{88,1... | collective-permute-start | bytes 6152 | tf_op jit(solution)/shard_map/ppermute | solution.py:189
  24.2 0.7 broadcast_multiply_fusion
  24.9 0.7 %concatenate.6 = s32[13]{0:T(128)S(1)} concatenate(s32[1]{0:T(128)} %bitcast, s32[1]{0:T(128)} %bitcast.1, s32[1]{0:T(128)} %bitcast.2, s32[1]{0:T(128)} %bitcast.3, s32[1]{0:T(128)} %bitcast.4, s32[4]{0:T(128)} %param.14, s32[4]{0:T(128)} %param.15), dimensions={0} | concatenate | bytes 104 | tf_op jit(solution)/shard_map/concatenate | solution.py:202
  25.6 3.1 %collective-permute-done.5 = bf16[2,4,128]{2,1,0:T(4,128)(2,1)S(1)} collective-permute-done((bf16[2,4,128]{2,1,0:T(4,128)(2,1)S(1)}, bf16[2,4,128]{2,1,0:T(4,128)(2,1)S(1)}, u32[]{:S(2)}, u32[]{:S(2)}) %collective-permute-start.5) | collective-permute-done | bytes 2080 | tf_op jit(solution)/shard_map/ppermute | solution.py:189
  28.8 1.0 %fusion.4 = (bf16[2,1,2,24,4,128]{5,4,3,2,1,0:T(4,128)(2,1)S(1)}, bf16[2,1,2,24,4,128]{5,4,3,2,1,0:T(4,128)(2,1)S(1)}) fusion(bf16[2,2,2,24,4,128]{5,4,3,2,1,0:T(4,128)(2,1)} %bitcast.18), kind=kLoop, calls=%fused_computation.14 | loop fusion | bytes 393216 | tf_op jit(solution)/shard_map/slice | solution.py:197
  29.8 1.1 %pad_maximum_fusion = (bf16[2,2,2,24,4,128]{5,4,3,2,1,0:T(4,128)(2,1)S(1)}, bf16[2,2,2,24,4,128]{5,4,3,2,1,0:T(4,128)(2,1)S(1)}) fusion(bf16[2,1,2,24,4,128]{5,4,3,2,1,0:T(4,128)(2,1)S(1)} %get-tuple-element.50, bf16[2,1,2,24,4,128]{5,4,3,2,1,0:T(4,128)(2,1)S(1)} %get-tuple-element.49, bf16[2,2,2,24,4,128]{5,4,3,2,1,0:T(4,128)(2,1)} %bitcast.19, pred[]{:T(512)S(6)} %eq.16), kind=kLoop, calls=%fused_computation.5 | loop fusion | flops 196608 | bytes 786433 | tf_op jit(solution)/shard_map/stack | solution.py:197
  30.9 0.1 fusion.3
  31.0 0.1 pad_maximum_fusion.1
  31.2 1.3 %collective-permute-start.6 = (bf16[2,4,128]{2,1,0:T(4,128)(2,1)S(1)}, bf16[2,4,128]{2,1,0:T(4,128)(2,1)S(1)}, u32[]{:S(2)}, u32[]{:S(2)}) collective-permute-start(bf16[2,4,128]{2,1,0:T(4,128)(2,1)S(1)} %add.52), channel_id=1, source_target_pairs={{0,256},{1,257},{2,258},{3,259},{4,260},{5,261},{6,262},{7,263},{8... | collective-permute-start | bytes 6152 | tf_op jit(solution)/shard_map/ppermute | solution.py:189
  32.6 0.7 collective-permute-done.6
  33.3 8.8 %all-to-all-done.halo_ref = bf16[8,2,192,128]{3,2,1,0:T(8,128)(2,1)S(1)} async-done(((bf16[8,2,192,128]{3,2,1,0:T(8,128)(2,1)}), bf16[8,2,192,128]{3,2,1,0:T(8,128)(2,1)S(1)}, u32[]{:S(2)}, u32[]{:S(2)}) %all-to-all-start) | async-done | bytes 786464 | tf_op jit(solution)/shard_map/all_to_all | solution.py:182
  42.0 0.1 broadcast_in_dim.20.table
  42.1 0.1 broadcast_in_dim.21.bias
  42.2 2.0 %attend.3 = bf16[96,512]{1,0:T(8,128)(2,1)S(1)} custom-call(s32[16,128]{1,0:T(8,128)S(1)} %broadcast_in_dim.20.table, f32[8,128]{1,0:T(8,128)S(1)} %broadcast_in_dim.21.bias, bf16[2,4,96,128]{3,2,1,0:T(8,128)(2,1)S(1)} %bitcast.16, bf16[8,2,192,128]{3,2,1,0:T(8,128)(2,1)S(1)} %all-to-all-done.halo_ref, bf16[2,256,128]{2,1,0:T(8,128)(2,1)S(1)} %fusion.2.near_ref), custom_call_target="tpu_custom_call" | custom-call | flops 2818572288 | bytes 786432 | tf_op jit(solution)/shard_map/attend/pallas_call | solution.py:107
  44.2 0.1 copy-done
  44.4 0.8 %convolution_convert_fusion = bf16[96,4096]{1,0:T(8,128)(2,1)S(1)} fusion(bf16[96,512]{1,0:T(8,128)(2,1)S(1)} %attend.3, bf16[512,4096]{1,0:T(8,128)(2,1)S(1)} %copy-done), kind=kOutput, calls=%fused_computation.1 | convolution fusion | flops 403046400 | bytes 5079040 | tf_op jit(solution)/shard_map/dot_general | solution.py:208
  45.2 2.5 %collective-permute-start.7 = (bf16[96,4096]{1,0:T(8,128)(2,1)S(1)}, bf16[96,4096]{1,0:T(8,128)(2,1)S(1)}, u32[]{:S(2)}, u32[]{:S(2)}) collective-permute-start(bf16[96,4096]{1,0:T(8,128)(2,1)S(1)} %convolution_convert_fusion), channel_id=1, source_target_pairs={{0,1},{1,0},{2,3},{3,2},{4,5},{5,4},{6,7},{7,6},{8,9},{9,8},{10,11... | collective-permute-start | bytes 2359304 | tf_op jit(solution)/shard_map/ppermute | solution.py:209
  47.7 2.0 %attend.2.rows_ref = bf16[96,512]{1,0:T(8,128)(2,1)S(1)} custom-call(s32[16,128]{1,0:T(8,128)S(1)} %broadcast_in_dim.20.table, f32[8,128]{1,0:T(8,128)S(1)} %broadcast_in_dim.21.bias, bf16[2,4,96,128]{3,2,1,0:T(8,128)(2,1)S(1)} %bitcast.17, bf16[8,2,192,128]{3,2,1,0:T(8,128)(2,1)S(1)} %all-to-all-done.halo_ref, bf16[2,256,128]{2,1,0:T(8,128)(2,1)S(1)} %fusion.2.near_ref), custom_call_target="tpu_custom_call" | custom-call | flops 2818572288 | bytes 786432 | tf_op jit(solution)/shard_map/attend/pallas_call | solution.py:107
  49.8 0.9 %project.1 = (bf16[24,4096]{1,0:T(8,128)(2,1)S(1)}, bf16[24,4096]{1,0:T(8,128)(2,1)S(1)}, bf16[24,4096]{1,0:T(8,128)(2,1)S(1)}, bf16[24,4096]{1,0:T(8,128)(2,1)S(1)}) custom-call(bf16[96,512]{1,0:T(8,128)(2,1)S(1)} %attend.2.rows_ref, bf16[512,4096]{1,0:T(8,128)(2,1)S(1)} %copy-done, bf16[96,4096]{1,0:T(8,128)(2,1)S(1)} %collective-permute-done.7.theirs_ref), custom_call_target="tpu_custom_call" | custom-call | flops 402653184 | bytes 4194304 | tf_op jit(solution)/shard_map/project/pallas_call | solution.py:142
  50.7 7.0 %collective-permute-start.10 = (bf16[24,4096]{1,0:T(8,128)(2,1)S(1)}, bf16[24,4096]{1,0:T(8,128)(2,1)S(1)}, u32[]{:S(2)}, u32[]{:S(2)}) collective-permute-start(bf16[24,4096]{1,0:T(8,128)(2,1)S(1)} %get-tuple-element.44), channel_id=1, source_target_pairs={{0,4},{2,6},{4,0},{6,2},{1,5},{3,7},{5,1},{7,3},{8,12},{10,14},{12... | collective-permute-start | bytes 589832 | tf_op jit(solution)/shard_map/ppermute | solution.py:215
  57.6 1.9 %collective-permute-start.9 = (bf16[24,4096]{1,0:T(8,128)(2,1)S(1)}, bf16[24,4096]{1,0:T(8,128)(2,1)S(1)}, u32[]{:S(2)}, u32[]{:S(2)}) collective-permute-start(bf16[24,4096]{1,0:T(8,128)(2,1)S(1)} %get-tuple-element.43), channel_id=1, source_target_pairs={{0,2},{2,0},{4,6},{6,4},{1,3},{3,1},{5,7},{7,5},{8,10},{10,8},{12,... | collective-permute-start | bytes 589832 | tf_op jit(solution)/shard_map/ppermute | solution.py:215
  59.6 3.1 %collective-permute-start.8 = (bf16[24,4096]{1,0:T(8,128)(2,1)S(1)}, bf16[24,4096]{1,0:T(8,128)(2,1)S(1)}, u32[]{:S(2)}, u32[]{:S(2)}) collective-permute-start(bf16[24,4096]{1,0:T(8,128)(2,1)S(1)} %get-tuple-element.42), channel_id=1, source_target_pairs={{0,6},{2,4},{4,2},{6,0},{1,7},{3,5},{5,3},{7,1},{8,14},{10,12},{12... | collective-permute-start | bytes 589832 | tf_op jit(solution)/shard_map/ppermute | solution.py:215
  62.7 2.8 %collective-permute-done.10 = bf16[24,4096]{1,0:T(8,128)(2,1)S(1)} collective-permute-done((bf16[24,4096]{1,0:T(8,128)(2,1)S(1)}, bf16[24,4096]{1,0:T(8,128)(2,1)S(1)}, u32[]{:S(2)}, u32[]{:S(2)}) %collective-permute-start.10) | collective-permute-done | bytes 196640 | tf_op jit(solution)/shard_map/ppermute | solution.py:215
  65.5 8.3 %collective-permute-done.9 = bf16[24,4096]{1,0:T(8,128)(2,1)S(1)} collective-permute-done((bf16[24,4096]{1,0:T(8,128)(2,1)S(1)}, bf16[24,4096]{1,0:T(8,128)(2,1)S(1)}, u32[]{:S(2)}, u32[]{:S(2)}) %collective-permute-start.9) | collective-permute-done | bytes 196640 | tf_op jit(solution)/shard_map/ppermute | solution.py:215
  73.8 0.8 %add_convert_fusion = bf16[24,4096]{1,0:T(8,128)(2,1)} fusion(bf16[24,4096]{1,0:T(8,128)(2,1)S(1)} %collective-permute-done.10, bf16[24,4096]{1,0:T(8,128)(2,1)S(1)} %collective-permute-done.9, bf16[24,4096]{1,0:T(8,128)(2,1)S(1)} %collective-permute-done.8, bf16[24,4096]{1,0:T(8,128)(2,1)S(1)} %get-tuple-element.41), kind=kLoop, calls=%fused_computation.2 | loop fusion | flops 786432 | bytes 983040 | tf_op jit(solution)/shard_map/convert_element_type | solution.py:216
  (18 shorter events, 0.2 us)
Async XLA Ops:
  0.0 32.5 %copy-start.1 = (bf16[192,4,128]{2,1,0:T(4,128)(2,1)S(1)}, bf16[192,4,128]{2,1,0:T(4,128)(2,1)}, u32[]{:S(2)}) copy-start(bf16[192,4,128]{2,1,0:T(4,128)(2,1)} %param.11) | copy-start | bytes 589828
  0.9 12.2 %collective-permute-start.3 = (bf16[2,192,128]{2,1,0:T(8,128)(2,1)S(1)}, bf16[2,192,128]{2,1,0:T(8,128)(2,1)S(1)}, u32[]{:S(2)}, u32[]{:S(2)}) collective-permute-start(bf16[2,192,128]{2,1,0:T(8,128)(2,1)S(1)} %pad_maximum_fusion.2.own_ref), channel_id=1, source_target_pairs={{0,64},{8,72},{16,80},{24,88},{32,96},{40,104},{48,112},{56,120},{... | collective-permute-start | bytes 294920 | tf_op jit(solution)/shard_map/ppermute | solution.py:176
  13.1 9.8 %collective-permute-start.4 = (bf16[2,4,128]{2,1,0:T(4,128)(2,1)S(1)}, bf16[2,4,128]{2,1,0:T(4,128)(2,1)S(1)}, u32[]{:S(2)}, u32[]{:S(2)}) collective-permute-start(bf16[2,4,128]{2,1,0:T(4,128)(2,1)S(1)} %get-tuple-element.52), channel_id=1, source_target_pairs={{0,64},{8,72},{16,80},{24,88},{32,96},{40,104},{48,112},{56,120},{... | collective-permute-start | bytes 6152 | tf_op jit(solution)/shard_map/ppermute | solution.py:189
  14.9 27.1 %all-to-all-start = ((bf16[8,2,192,128]{3,2,1,0:T(8,128)(2,1)}), bf16[8,2,192,128]{3,2,1,0:T(8,128)(2,1)S(1)}, u32[]{:S(2)}, u32[]{:S(2)}) async-start(bf16[8,2,192,128]{3,2,1,0:T(8,128)(2,1)} %pack.1), calls=%async_computation | async-start | bytes 1572864 | tf_op jit(solution)/shard_map/all_to_all | solution.py:182
  22.9 5.8 %collective-permute-start.5 = (bf16[2,4,128]{2,1,0:T(4,128)(2,1)S(1)}, bf16[2,4,128]{2,1,0:T(4,128)(2,1)S(1)}, u32[]{:S(2)}, u32[]{:S(2)}) collective-permute-start(bf16[2,4,128]{2,1,0:T(4,128)(2,1)S(1)} %add.51), channel_id=1, source_target_pairs={{0,192},{64,128},{8,200},{72,136},{16,208},{80,144},{24,216},{88,1... | collective-permute-start | bytes 6152 | tf_op jit(solution)/shard_map/ppermute | solution.py:189
  31.2 2.0 %collective-permute-start.6 = (bf16[2,4,128]{2,1,0:T(4,128)(2,1)S(1)}, bf16[2,4,128]{2,1,0:T(4,128)(2,1)S(1)}, u32[]{:S(2)}, u32[]{:S(2)}) collective-permute-start(bf16[2,4,128]{2,1,0:T(4,128)(2,1)S(1)} %add.52), channel_id=1, source_target_pairs={{0,256},{1,257},{2,258},{3,259},{4,260},{5,261},{6,262},{7,263},{8... | collective-permute-start | bytes 6152 | tf_op jit(solution)/shard_map/ppermute | solution.py:189
  42.2 2.2 %copy-start = (bf16[512,4096]{1,0:T(8,128)(2,1)S(1)}, bf16[512,4096]{1,0:T(8,128)(2,1)}, u32[]{:S(2)}) copy-start(bf16[512,4096]{1,0:T(8,128)(2,1)} %weight_ref.1) | copy-start | bytes 12582916
  45.2 4.6 %collective-permute-start.7 = (bf16[96,4096]{1,0:T(8,128)(2,1)S(1)}, bf16[96,4096]{1,0:T(8,128)(2,1)S(1)}, u32[]{:S(2)}, u32[]{:S(2)}) collective-permute-start(bf16[96,4096]{1,0:T(8,128)(2,1)S(1)} %convolution_convert_fusion), channel_id=1, source_target_pairs={{0,1},{1,0},{2,3},{3,2},{4,5},{5,4},{6,7},{7,6},{8,9},{9,8},{10,11... | collective-permute-start | bytes 2359304 | tf_op jit(solution)/shard_map/ppermute | solution.py:209
  50.7 14.9 %collective-permute-start.10 = (bf16[24,4096]{1,0:T(8,128)(2,1)S(1)}, bf16[24,4096]{1,0:T(8,128)(2,1)S(1)}, u32[]{:S(2)}, u32[]{:S(2)}) collective-permute-start(bf16[24,4096]{1,0:T(8,128)(2,1)S(1)} %get-tuple-element.44), channel_id=1, source_target_pairs={{0,4},{2,6},{4,0},{6,2},{1,5},{3,7},{5,1},{7,3},{8,12},{10,14},{12... | collective-permute-start | bytes 589832 | tf_op jit(solution)/shard_map/ppermute | solution.py:215
  57.6 16.2 %collective-permute-start.9 = (bf16[24,4096]{1,0:T(8,128)(2,1)S(1)}, bf16[24,4096]{1,0:T(8,128)(2,1)S(1)}, u32[]{:S(2)}, u32[]{:S(2)}) collective-permute-start(bf16[24,4096]{1,0:T(8,128)(2,1)S(1)} %get-tuple-element.43), channel_id=1, source_target_pairs={{0,2},{2,0},{4,6},{6,4},{1,3},{3,1},{5,7},{7,5},{8,10},{10,8},{12,... | collective-permute-start | bytes 589832 | tf_op jit(solution)/shard_map/ppermute | solution.py:215
  59.6 14.3 %collective-permute-start.8 = (bf16[24,4096]{1,0:T(8,128)(2,1)S(1)}, bf16[24,4096]{1,0:T(8,128)(2,1)S(1)}, u32[]{:S(2)}, u32[]{:S(2)}) collective-permute-start(bf16[24,4096]{1,0:T(8,128)(2,1)S(1)} %get-tuple-element.42), channel_id=1, source_target_pairs={{0,6},{2,4},{4,2},{6,0},{1,7},{3,5},{5,3},{7,1},{8,14},{10,12},{12... | collective-permute-start | bytes 589832 | tf_op jit(solution)/shard_map/ppermute | solution.py:215

commit v4 on v3

--- a/solution.py
+++ b/solution.py
@@ -30,24 +30,33 @@
     return sum(jnp.where(number == k, y, 0) for k, y in enumerate(ORDER))
 
 
-def pack_kernel(y_ref, own_ref, before_ref, sent_ref):
-    target = listed(lax.broadcasted_iota(jnp.int32, y_ref.shape, 0))
-    later = (target > y_ref[...]).astype(jnp.float32).astype(jnp.bfloat16)
-    for number in range(sent_ref.shape[0]):
-        chosen = later[number : number + 1]
-        sent_ref[number] = own_ref[...] * chosen + before_ref[...] * (1 - chosen)
-
-
-def pack(y, own, before, row_len):
+def pack_kernel(own_ref, before_ref, sent_ref, done):
+    y = lax.axis_index("y")
+    for number, target in enumerate(ORDER):
+
+        @pl.when(target > y)
+        def _():
+            pltpu.make_async_copy(own_ref, sent_ref.at[number], done.at[number]).start()
+
+        @pl.when(target <= y)
+        def _():
+            pltpu.make_async_copy(before_ref, sent_ref.at[number], done.at[number]).start()
+
+    for number in range(len(ORDER)):
+        pltpu.make_async_copy(own_ref, sent_ref.at[number], done.at[number]).wait()
+
+
+def pack(own, before, row_len):
     vmem = pl.BlockSpec(memory_space=pltpu.VMEM)
     return pl.pallas_call(
         pack_kernel,
         out_shape=jax.ShapeDtypeStruct((row_len, *own.shape), own.dtype),
-        in_specs=[vmem] * 3,
-        out_specs=vmem,
+        in_specs=[vmem] * 2,
+        out_specs=pl.BlockSpec(memory_space=pl.ANY),
+        scratch_shapes=[pltpu.SemaphoreType.DMA((row_len,))],
         compiler_params=pltpu.CompilerParams(vmem_limit_bytes=8 << 20),
         name="pack",
-    )(jnp.full((row_len, LANES), y, jnp.int32), own, before)
+    )(own, before)
 
 
 def attend_kernel(
@@ -74,29 +83,36 @@
     q = (q_ref[0] * first + q_ref[1] * (1 - first)).reshape(heads * rows, width)
     transposed = (((1,), (1,)), ((), ()))
     keys = jnp.concatenate([halo_ref[:, 0].reshape(halo_len, width), near_ref[0]], axis=0)
-    score_ref[...] = lax.dot_general(q, keys, transposed, preferred_element_type=jnp.float32)
-    totals = []
-    for h in range(heads):
-        window, count = (table[k : k + 1, :1] for k in (5 + h, 5 + heads + h))
-        lowest = jnp.maximum(query_pos - window + 1, count)
-        ranked = jnp.where(is_sink, jnp.where(near_pos < count, ALWAYS, NEVER), near_pos)
-        mine = slice(h * rows, (h + 1) * rows)
-        far = jnp.where(halo_pos >= lowest, score_ref[mine, :halo_len], NEG)
-        close = score_ref[mine, halo_len:] + jnp.where(is_sink, bias[h : h + 1, :1], 0.0)
-        close = jnp.where((near_pos <= query_pos) & (ranked >= lowest), close, NEG)
-        top = jnp.maximum(
-            jnp.max(far, axis=1, keepdims=True), jnp.max(close, axis=1, keepdims=True)
+    values = jnp.concatenate([halo_ref[:, 1].reshape(halo_len, width), near_ref[1]], axis=0)
+    for pair in range(0, heads, 2):
+        both = slice(pair * rows, (pair + 2) * rows)
+        score_ref[both] = lax.dot_general(
+            q[both], keys, transposed, preferred_element_type=jnp.float32
         )
-        far = jnp.exp2((far - top) * unit)
-        close = jnp.exp2((close - top) * unit)
-        totals.append(jnp.sum(far, axis=1, keepdims=True) + jnp.sum(close, axis=1, keepdims=True))
-        prob_ref[mine, :halo_len] = far.astype(jnp.bfloat16)
-        prob_ref[mine, halo_len:] = close.astype(jnp.bfloat16)
-    values = jnp.concatenate([halo_ref[:, 1].reshape(halo_len, width), near_ref[1]], axis=0)
-    mixed = jnp.dot(prob_ref[...], values, preferred_element_type=jnp.float32)
-    for h in range(heads):
-        block = mixed[h * rows : (h + 1) * rows] / totals[h]
-        out_ref[:, h * width : (h + 1) * width] = block.astype(out_ref.dtype)
+        totals = []
+        for h in range(pair, pair + 2):
+            window, count = (table[k : k + 1, :1] for k in (5 + h, 5 + heads + h))
+            lowest = jnp.maximum(query_pos - window + 1, count)
+            ranked = jnp.where(is_sink, jnp.where(near_pos < count, ALWAYS, NEVER), near_pos)
+            mine = slice(h * rows, (h + 1) * rows)
+            far = jnp.where(halo_pos >= lowest, score_ref[mine, :halo_len], NEG)
+            close = score_ref[mine, halo_len:] + jnp.where(is_sink, bias[h : h + 1, :1], 0.0)
+            close = jnp.where((near_pos <= query_pos) & (ranked >= lowest), close, NEG)
+            top = jnp.maximum(
+                jnp.max(far, axis=1, keepdims=True), jnp.max(close, axis=1, keepdims=True)
+            )
+            far = jnp.exp2((far - top) * unit)
+            close = jnp.exp2((close - top) * unit)
+            totals.append(
+                jnp.sum(far, axis=1, keepdims=True) + jnp.sum(close, axis=1, keepdims=True)
+            )
+            prob_ref[mine, :halo_len] = far.astype(jnp.bfloat16)
+            prob_ref[mine, halo_len:] = close.astype(jnp.bfloat16)
+        mixed = jnp.dot(prob_ref[both], values, preferred_element_type=jnp.float32)
+        for h in range(2):
+            block = mixed[h * rows : (h + 1) * rows] / totals[h]
+            first_lane = (pair + h) * width
+            out_ref[:, first_lane : first_lane + width] = block.astype(out_ref.dtype)
 
 
 def attend(number, table, sink_bias, q, halo, near):
@@ -178,7 +194,7 @@
         first_row, lambda v: along_row(SPREAD[1:3], v), lambda v: v, sinks
     )
     before, sinks = lax.optimization_barrier((before, sinks))
-    sent = pack(y, stacked, before, row_len)
+    sent = pack(stacked, before, row_len)
     halo = lax.all_to_all(sent, "y", 0, 0, axis_index_groups=[list(ORDER)], tiled=True)
     windows, sink_counts, sink_bias, _ = lax.optimization_barrier(
         (windows, sink_counts, sink_bias, sent)

time: 75.1 us -> 74.8 us (level)
  Pallas kernels: 6.07 us -> 5.08 us
    pallas_call x2, Pallas kernels: 4.09 us -> 3.24 us  [attend(): pl.pallas_call(functools.partial(attend_kernel, tok_rows=tok_rows, number...]
  transfers between devices with their start and end apart: 9 -> 9, of which waited for: 6 -> 7; matrix products, arithmetic and copies ran while one was open for 5% -> 5% of each run, Pallas kernels for 4% -> 3%
where the time goes in v4:
time: 74.8 us; the launch traced here: 74.3 us
  starting transfers between devices  36.3 us (49%)
  waiting for transfers between devices  25.6 us (34%)
  Pallas kernels  5.08 us (7%)
  other arithmetic  3.67 us (5%)
  local copies, waits for them, and re-layouts  2.61 us (3%)
  matrix products  0.83 us (1%)
    ppermute x3, starting transfers between devices, shards(): total += lax.ppermute(parts[distance], 'zl', route).astype(jnp.float32)  12 us
    ppermute x3, waiting for transfers between devices, shards(): total += lax.ppermute(parts[distance], 'zl', route).astype(jnp.float32)  11.2 us
    ppermute x1, starting transfers between devices, shards(): lax.ppermute(stacked, SEQ, [(i, i + row_len) for i in range(seq_len - row...  10.6 us
    all_to_all x1, waiting for transfers between devices, shards(): lax.all_to_all(sent, 'y', 0, 0, axis_index_groups=[list(ORDER)], tiled=True)  8.78 us
    all_to_all x1, starting transfers between devices, shards(): lax.all_to_all(sent, 'y', 0, 0, axis_index_groups=[list(ORDER)], tiled=True)  8.03 us
    ppermute x3, waiting for transfers between devices, shards(): sinks = sinks + lax.ppermute(sinks, axis, route)  3.77 us
    pallas_call x2, Pallas kernels, attend(): pl.pallas_call(functools.partial(attend_kernel, tok_rows=tok_rows, number...  3.24 us
    ppermute x3, starting transfers between devices, shards(): sinks = sinks + lax.ppermute(sinks, axis, route)  3.23 us
  transfers between devices with their start and end apart: 9, of which 7 were waited for; matrix products, arithmetic and copies ran while one was open for 5% of the time, Pallas kernels for 3%

profile of v4, /device:TPU:15, one launch (start us, length us, event | category | flops | bytes accessed | tf_op | source)
XLA Modules:
  0.0 74.3 jit_solution(5775917018302085882)
XLA Ops:
  0.0 0.9 %pad_maximum_fusion.2.own_ref = bf16[2,192,128]{2,1,0:T(8,128)(2,1)S(1)} fusion(bf16[1,192,128]{2,1,0:T(8,128)(2,1)} %bitcast.23, bf16[1,192,128]{2,1,0:T(8,128)(2,1)} %bitcast.24), kind=kLoop, calls=%fused_computation.11 | loop fusion | flops 49152 | bytes 196608 | tf_op jit(solution)/shard_map/stack | solution.py:177
  0.9 10.6 %collective-permute-start.3 = (bf16[2,192,128]{2,1,0:T(8,128)(2,1)S(1)}, bf16[2,192,128]{2,1,0:T(8,128)(2,1)S(1)}, u32[]{:S(2)}, u32[]{:S(2)}) collective-permute-start(bf16[2,192,128]{2,1,0:T(8,128)(2,1)S(1)} %pad_maximum_fusion.2.own_ref), channel_id=1, source_target_pairs={{0,64},{8,72},{16,80},{24,88},{32,96},{40,104},{48,112},{56,120},{... | collective-permute-start | bytes 294920 | tf_op jit(solution)/shard_map/ppermute | solution.py:192
  11.5 1.6 %collective-permute-done.3.before_ref = bf16[2,192,128]{2,1,0:T(8,128)(2,1)S(1)} collective-permute-done((bf16[2,192,128]{2,1,0:T(8,128)(2,1)S(1)}, bf16[2,192,128]{2,1,0:T(8,128)(2,1)S(1)}, u32[]{:S(2)}, u32[]{:S(2)}) %collective-permute-start.3) | collective-permute-done | bytes 98336 | tf_op jit(solution)/shard_map/ppermute | solution.py:192
  13.1 0.6 collective-permute-start.4
  13.8 1.0 %pack.1 = bf16[8,2,192,128]{3,2,1,0:T(8,128)(2,1)} custom-call(bf16[2,192,128]{2,1,0:T(8,128)(2,1)S(1)} %pad_maximum_fusion.2.own_ref, bf16[2,192,128]{2,1,0:T(8,128)(2,1)S(1)} %collective-permute-done.3.before_ref), custom_call_target="tpu_custom_call" | custom-call | tf_op jit(solution)/shard_map/pack/pallas_call | solution.py:51
  14.8 8.0 %all-to-all-start = ((bf16[8,2,192,128]{3,2,1,0:T(8,128)(2,1)}), bf16[8,2,192,128]{3,2,1,0:T(8,128)(2,1)S(1)}, u32[]{:S(2)}, u32[]{:S(2)}) async-start(bf16[8,2,192,128]{3,2,1,0:T(8,128)(2,1)} %pack.1), calls=%async_computation | async-start | bytes 1572864 | tf_op jit(solution)/shard_map/all_to_all | solution.py:198
  22.8 1.3 %collective-permute-start.5 = (bf16[2,4,128]{2,1,0:T(4,128)(2,1)S(1)}, bf16[2,4,128]{2,1,0:T(4,128)(2,1)S(1)}, u32[]{:S(2)}, u32[]{:S(2)}) collective-permute-start(bf16[2,4,128]{2,1,0:T(4,128)(2,1)S(1)} %add.51), channel_id=1, source_target_pairs={{0,192},{64,128},{8,200},{72,136},{16,208},{80,144},{24,216},{88,1... | collective-permute-start | bytes 6152 | tf_op jit(solution)/shard_map/ppermute | solution.py:205
  24.1 0.7 broadcast_multiply_fusion
  24.8 0.7 %concatenate.6 = s32[13]{0:T(128)S(1)} concatenate(s32[1]{0:T(128)} %bitcast, s32[1]{0:T(128)} %bitcast.1, s32[1]{0:T(128)} %bitcast.2, s32[1]{0:T(128)} %bitcast.3, s32[1]{0:T(128)} %bitcast.4, s32[4]{0:T(128)} %param.14, s32[4]{0:T(128)} %param.15), dimensions={0} | concatenate | bytes 104 | tf_op jit(solution)/shard_map/concatenate | solution.py:218
  25.5 3.1 %collective-permute-done.5 = bf16[2,4,128]{2,1,0:T(4,128)(2,1)S(1)} collective-permute-done((bf16[2,4,128]{2,1,0:T(4,128)(2,1)S(1)}, bf16[2,4,128]{2,1,0:T(4,128)(2,1)S(1)}, u32[]{:S(2)}, u32[]{:S(2)}) %collective-permute-start.5) | collective-permute-done | bytes 2080 | tf_op jit(solution)/shard_map/ppermute | solution.py:205
  28.6 1.0 %fusion.4 = (bf16[2,1,2,24,4,128]{5,4,3,2,1,0:T(4,128)(2,1)S(1)}, bf16[2,1,2,24,4,128]{5,4,3,2,1,0:T(4,128)(2,1)S(1)}) fusion(bf16[2,2,2,24,4,128]{5,4,3,2,1,0:T(4,128)(2,1)} %bitcast.18), kind=kLoop, calls=%fused_computation.14 | loop fusion | bytes 393216 | tf_op jit(solution)/shard_map/slice | solution.py:213
  29.6 1.1 %pad_maximum_fusion = (bf16[2,2,2,24,4,128]{5,4,3,2,1,0:T(4,128)(2,1)S(1)}, bf16[2,2,2,24,4,128]{5,4,3,2,1,0:T(4,128)(2,1)S(1)}) fusion(bf16[2,1,2,24,4,128]{5,4,3,2,1,0:T(4,128)(2,1)S(1)} %get-tuple-element.50, bf16[2,1,2,24,4,128]{5,4,3,2,1,0:T(4,128)(2,1)S(1)} %get-tuple-element.49, bf16[2,2,2,24,4,128]{5,4,3,2,1,0:T(4,128)(2,1)} %bitcast.19, pred[]{:T(512)S(6)} %eq.16), kind=kLoop, calls=%fused_computation.5 | loop fusion | flops 196608 | bytes 786433 | tf_op jit(solution)/shard_map/stack | solution.py:213
  30.8 0.1 fusion.3
  30.9 0.1 pad_maximum_fusion.1
  31.1 1.3 %collective-permute-start.6 = (bf16[2,4,128]{2,1,0:T(4,128)(2,1)S(1)}, bf16[2,4,128]{2,1,0:T(4,128)(2,1)S(1)}, u32[]{:S(2)}, u32[]{:S(2)}) collective-permute-start(bf16[2,4,128]{2,1,0:T(4,128)(2,1)S(1)} %add.52), channel_id=1, source_target_pairs={{0,256},{1,257},{2,258},{3,259},{4,260},{5,261},{6,262},{7,263},{8... | collective-permute-start | bytes 6152 | tf_op jit(solution)/shard_map/ppermute | solution.py:205
  32.5 0.7 collective-permute-done.6
  33.1 8.8 %all-to-all-done.halo_ref = bf16[8,2,192,128]{3,2,1,0:T(8,128)(2,1)S(1)} async-done(((bf16[8,2,192,128]{3,2,1,0:T(8,128)(2,1)}), bf16[8,2,192,128]{3,2,1,0:T(8,128)(2,1)S(1)}, u32[]{:S(2)}, u32[]{:S(2)}) %all-to-all-start) | async-done | bytes 786464 | tf_op jit(solution)/shard_map/all_to_all | solution.py:198
  41.9 0.1 broadcast_in_dim.8.table
  42.0 0.1 broadcast_in_dim.9.bias
  42.0 1.6 %attend.3 = bf16[96,512]{1,0:T(8,128)(2,1)S(1)} custom-call(s32[16,128]{1,0:T(8,128)S(1)} %broadcast_in_dim.8.table, f32[8,128]{1,0:T(8,128)S(1)} %broadcast_in_dim.9.bias, bf16[2,4,96,128]{3,2,1,0:T(8,128)(2,1)S(1)} %bitcast.16, bf16[8,2,192,128]{3,2,1,0:T(8,128)(2,1)S(1)} %all-to-all-done.halo_ref, bf16[2,256,128]{2,1,0:T(8,128)(2,1)S(1)} %fusion.2.near_ref), custom_call_target="tpu_custom_call" | custom-call | flops 2818572288 | bytes 786432 | tf_op jit(solution)/shard_map/attend/pallas_call | solution.py:123
  43.7 0.6 copy-done
  44.2 0.8 %convolution_convert_fusion = bf16[96,4096]{1,0:T(8,128)(2,1)S(1)} fusion(bf16[96,512]{1,0:T(8,128)(2,1)S(1)} %attend.3, bf16[512,4096]{1,0:T(8,128)(2,1)S(1)} %copy-done), kind=kOutput, calls=%fused_computation.1 | convolution fusion | flops 403046400 | bytes 5079040 | tf_op jit(solution)/shard_map/dot_general | solution.py:224
  45.1 2.5 %collective-permute-start.7 = (bf16[96,4096]{1,0:T(8,128)(2,1)S(1)}, bf16[96,4096]{1,0:T(8,128)(2,1)S(1)}, u32[]{:S(2)}, u32[]{:S(2)}) collective-permute-start(bf16[96,4096]{1,0:T(8,128)(2,1)S(1)} %convolution_convert_fusion), channel_id=1, source_target_pairs={{0,1},{1,0},{2,3},{3,2},{4,5},{5,4},{6,7},{7,6},{8,9},{9,8},{10,11... | collective-permute-start | bytes 2359304 | tf_op jit(solution)/shard_map/ppermute | solution.py:225
  47.6 1.6 %attend.2.rows_ref = bf16[96,512]{1,0:T(8,128)(2,1)S(1)} custom-call(s32[16,128]{1,0:T(8,128)S(1)} %broadcast_in_dim.8.table, f32[8,128]{1,0:T(8,128)S(1)} %broadcast_in_dim.9.bias, bf16[2,4,96,128]{3,2,1,0:T(8,128)(2,1)S(1)} %bitcast.17, bf16[8,2,192,128]{3,2,1,0:T(8,128)(2,1)S(1)} %all-to-all-done.halo_ref, bf16[2,256,128]{2,1,0:T(8,128)(2,1)S(1)} %fusion.2.near_ref), custom_call_target="tpu_custom_call" | custom-call | flops 2818572288 | bytes 786432 | tf_op jit(solution)/shard_map/attend/pallas_call | solution.py:123
  49.2 0.3 collective-permute-done.7.theirs_ref
  49.5 0.9 %project.1 = (bf16[24,4096]{1,0:T(8,128)(2,1)S(1)}, bf16[24,4096]{1,0:T(8,128)(2,1)S(1)}, bf16[24,4096]{1,0:T(8,128)(2,1)S(1)}, bf16[24,4096]{1,0:T(8,128)(2,1)S(1)}) custom-call(bf16[96,512]{1,0:T(8,128)(2,1)S(1)} %attend.2.rows_ref, bf16[512,4096]{1,0:T(8,128)(2,1)S(1)} %copy-done, bf16[96,4096]{1,0:T(8,128)(2,1)S(1)} %collective-permute-done.7.theirs_ref), custom_call_target="tpu_custom_call" | custom-call | flops 402653184 | bytes 4194304 | tf_op jit(solution)/shard_map/project/pallas_call | solution.py:158
  50.3 7.0 %collective-permute-start.10 = (bf16[24,4096]{1,0:T(8,128)(2,1)S(1)}, bf16[24,4096]{1,0:T(8,128)(2,1)S(1)}, u32[]{:S(2)}, u32[]{:S(2)}) collective-permute-start(bf16[24,4096]{1,0:T(8,128)(2,1)S(1)} %get-tuple-element.44), channel_id=1, source_target_pairs={{0,4},{2,6},{4,0},{6,2},{1,5},{3,7},{5,1},{7,3},{8,12},{10,14},{12... | collective-permute-start | bytes 589832 | tf_op jit(solution)/shard_map/ppermute | solution.py:231
  57.3 1.9 %collective-permute-start.9 = (bf16[24,4096]{1,0:T(8,128)(2,1)S(1)}, bf16[24,4096]{1,0:T(8,128)(2,1)S(1)}, u32[]{:S(2)}, u32[]{:S(2)}) collective-permute-start(bf16[24,4096]{1,0:T(8,128)(2,1)S(1)} %get-tuple-element.43), channel_id=1, source_target_pairs={{0,2},{2,0},{4,6},{6,4},{1,3},{3,1},{5,7},{7,5},{8,10},{10,8},{12,... | collective-permute-start | bytes 589832 | tf_op jit(solution)/shard_map/ppermute | solution.py:231
  59.3 3.1 %collective-permute-start.8 = (bf16[24,4096]{1,0:T(8,128)(2,1)S(1)}, bf16[24,4096]{1,0:T(8,128)(2,1)S(1)}, u32[]{:S(2)}, u32[]{:S(2)}) collective-permute-start(bf16[24,4096]{1,0:T(8,128)(2,1)S(1)} %get-tuple-element.42), channel_id=1, source_target_pairs={{0,6},{2,4},{4,2},{6,0},{1,7},{3,5},{5,3},{7,1},{8,14},{10,12},{12... | collective-permute-start | bytes 589832 | tf_op jit(solution)/shard_map/ppermute | solution.py:231
  62.4 2.8 %collective-permute-done.10 = bf16[24,4096]{1,0:T(8,128)(2,1)S(1)} collective-permute-done((bf16[24,4096]{1,0:T(8,128)(2,1)S(1)}, bf16[24,4096]{1,0:T(8,128)(2,1)S(1)}, u32[]{:S(2)}, u32[]{:S(2)}) %collective-permute-start.10) | collective-permute-done | bytes 196640 | tf_op jit(solution)/shard_map/ppermute | solution.py:231
  65.2 8.3 %collective-permute-done.9 = bf16[24,4096]{1,0:T(8,128)(2,1)S(1)} collective-permute-done((bf16[24,4096]{1,0:T(8,128)(2,1)S(1)}, bf16[24,4096]{1,0:T(8,128)(2,1)S(1)}, u32[]{:S(2)}, u32[]{:S(2)}) %collective-permute-start.9) | collective-permute-done | bytes 196640 | tf_op jit(solution)/shard_map/ppermute | solution.py:231
  73.5 0.8 %add_convert_fusion = bf16[24,4096]{1,0:T(8,128)(2,1)} fusion(bf16[24,4096]{1,0:T(8,128)(2,1)S(1)} %collective-permute-done.10, bf16[24,4096]{1,0:T(8,128)(2,1)S(1)} %collective-permute-done.9, bf16[24,4096]{1,0:T(8,128)(2,1)S(1)} %collective-permute-done.8, bf16[24,4096]{1,0:T(8,128)(2,1)S(1)} %get-tuple-element.41), kind=kLoop, calls=%fused_computation.2 | loop fusion | flops 786432 | bytes 983040 | tf_op jit(solution)/shard_map/convert_element_type | solution.py:232
  (17 shorter events, 0.2 us)
Async XLA Ops:
  0.0 32.4 %copy-start.1 = (bf16[192,4,128]{2,1,0:T(4,128)(2,1)S(1)}, bf16[192,4,128]{2,1,0:T(4,128)(2,1)}, u32[]{:S(2)}) copy-start(bf16[192,4,128]{2,1,0:T(4,128)(2,1)} %param.11) | copy-start | bytes 589828
  0.9 12.2 %collective-permute-start.3 = (bf16[2,192,128]{2,1,0:T(8,128)(2,1)S(1)}, bf16[2,192,128]{2,1,0:T(8,128)(2,1)S(1)}, u32[]{:S(2)}, u32[]{:S(2)}) collective-permute-start(bf16[2,192,128]{2,1,0:T(8,128)(2,1)S(1)} %pad_maximum_fusion.2.own_ref), channel_id=1, source_target_pairs={{0,64},{8,72},{16,80},{24,88},{32,96},{40,104},{48,112},{56,120},{... | collective-permute-start | bytes 294920 | tf_op jit(solution)/shard_map/ppermute | solution.py:192
  13.1 9.7 %collective-permute-start.4 = (bf16[2,4,128]{2,1,0:T(4,128)(2,1)S(1)}, bf16[2,4,128]{2,1,0:T(4,128)(2,1)S(1)}, u32[]{:S(2)}, u32[]{:S(2)}) collective-permute-start(bf16[2,4,128]{2,1,0:T(4,128)(2,1)S(1)} %get-tuple-element.52), channel_id=1, source_target_pairs={{0,64},{8,72},{16,80},{24,88},{32,96},{40,104},{48,112},{56,120},{... | collective-permute-start | bytes 6152 | tf_op jit(solution)/shard_map/ppermute | solution.py:205
  14.8 27.1 %all-to-all-start = ((bf16[8,2,192,128]{3,2,1,0:T(8,128)(2,1)}), bf16[8,2,192,128]{3,2,1,0:T(8,128)(2,1)S(1)}, u32[]{:S(2)}, u32[]{:S(2)}) async-start(bf16[8,2,192,128]{3,2,1,0:T(8,128)(2,1)} %pack.1), calls=%async_computation | async-start | bytes 1572864 | tf_op jit(solution)/shard_map/all_to_all | solution.py:198
  22.8 5.8 %collective-permute-start.5 = (bf16[2,4,128]{2,1,0:T(4,128)(2,1)S(1)}, bf16[2,4,128]{2,1,0:T(4,128)(2,1)S(1)}, u32[]{:S(2)}, u32[]{:S(2)}) collective-permute-start(bf16[2,4,128]{2,1,0:T(4,128)(2,1)S(1)} %add.51), channel_id=1, source_target_pairs={{0,192},{64,128},{8,200},{72,136},{16,208},{80,144},{24,216},{88,1... | collective-permute-start | bytes 6152 | tf_op jit(solution)/shard_map/ppermute | solution.py:205
  31.1 2.0 %collective-permute-start.6 = (bf16[2,4,128]{2,1,0:T(4,128)(2,1)S(1)}, bf16[2,4,128]{2,1,0:T(4,128)(2,1)S(1)}, u32[]{:S(2)}, u32[]{:S(2)}) collective-permute-start(bf16[2,4,128]{2,1,0:T(4,128)(2,1)S(1)} %add.52), channel_id=1, source_target_pairs={{0,256},{1,257},{2,258},{3,259},{4,260},{5,261},{6,262},{7,263},{8... | collective-permute-start | bytes 6152 | tf_op jit(solution)/shard_map/ppermute | solution.py:205
  42.0 2.2 %copy-start = (bf16[512,4096]{1,0:T(8,128)(2,1)S(1)}, bf16[512,4096]{1,0:T(8,128)(2,1)}, u32[]{:S(2)}) copy-start(bf16[512,4096]{1,0:T(8,128)(2,1)} %weight_ref.1) | copy-start | bytes 12582916
  45.1 4.4 %collective-permute-start.7 = (bf16[96,4096]{1,0:T(8,128)(2,1)S(1)}, bf16[96,4096]{1,0:T(8,128)(2,1)S(1)}, u32[]{:S(2)}, u32[]{:S(2)}) collective-permute-start(bf16[96,4096]{1,0:T(8,128)(2,1)S(1)} %convolution_convert_fusion), channel_id=1, source_target_pairs={{0,1},{1,0},{2,3},{3,2},{4,5},{5,4},{6,7},{7,6},{8,9},{9,8},{10,11... | collective-permute-start | bytes 2359304 | tf_op jit(solution)/shard_map/ppermute | solution.py:225
  50.3 14.8 %collective-permute-start.10 = (bf16[24,4096]{1,0:T(8,128)(2,1)S(1)}, bf16[24,4096]{1,0:T(8,128)(2,1)S(1)}, u32[]{:S(2)}, u32[]{:S(2)}) collective-permute-start(bf16[24,4096]{1,0:T(8,128)(2,1)S(1)} %get-tuple-element.44), channel_id=1, source_target_pairs={{0,4},{2,6},{4,0},{6,2},{1,5},{3,7},{5,1},{7,3},{8,12},{10,14},{12... | collective-permute-start | bytes 589832 | tf_op jit(solution)/shard_map/ppermute | solution.py:231
  57.3 16.2 %collective-permute-start.9 = (bf16[24,4096]{1,0:T(8,128)(2,1)S(1)}, bf16[24,4096]{1,0:T(8,128)(2,1)S(1)}, u32[]{:S(2)}, u32[]{:S(2)}) collective-permute-start(bf16[24,4096]{1,0:T(8,128)(2,1)S(1)} %get-tuple-element.43), channel_id=1, source_target_pairs={{0,2},{2,0},{4,6},{6,4},{1,3},{3,1},{5,7},{7,5},{8,10},{10,8},{12,... | collective-permute-start | bytes 589832 | tf_op jit(solution)/shard_map/ppermute | solution.py:231
  59.3 14.3 %collective-permute-start.8 = (bf16[24,4096]{1,0:T(8,128)(2,1)S(1)}, bf16[24,4096]{1,0:T(8,128)(2,1)S(1)}, u32[]{:S(2)}, u32[]{:S(2)}) collective-permute-start(bf16[24,4096]{1,0:T(8,128)(2,1)S(1)} %get-tuple-element.42), channel_id=1, source_target_pairs={{0,6},{2,4},{4,2},{6,0},{1,7},{3,5},{5,3},{7,1},{8,14},{10,12},{12... | collective-permute-start | bytes 589832 | tf_op jit(solution)/shard_map/ppermute | solution.py:231

commit v5 on v4

--- a/solution.py
+++ b/solution.py
@@ -22,7 +22,7 @@
     (SEQ, [(i + j, i + k) for i in range(8) for j, k in ((0, 24), (8, 16))]),
     ("zh", [(0, 1)]),
 )
-ORDER = (4, 5, 6, 7, 3, 2, 1, 0)
+ORDER = (5, 4, 3, 2, 6, 7, 0, 1)
 ALWAYS, NEVER = 1 << 30, -(1 << 30)
 
 
@@ -200,7 +200,7 @@
         (windows, sink_counts, sink_bias, sent)
     )
     for number, (axis, route) in enumerate(SPREAD[3:], 3):
-        if number == len(SPREAD) - 1:
+        if number == len(SPREAD) - 2:
             sinks, queries = lax.optimization_barrier((sinks, queries))
         sinks = sinks + lax.ppermute(sinks, axis, route)
     near = jnp.concatenate(
@@ -226,7 +226,7 @@
     mine = attend(1, table, bias, q, halo, near)
     parts = project(mine, out_weight, theirs, members)
     total = parts[0].astype(jnp.float32)
-    for distance in (3, 1, 2):
+    for distance in (2, 1, 3):
         route = [(i, i ^ distance) for i in range(members)]
         total += lax.ppermute(parts[distance], "zl", route).astype(jnp.float32)
     return total.astype(jnp.bfloat16)

time: 74.8 us -> 74.6 us (level)
  the two profiles are of different devices: /device:TPU:15 before, /device:TPU:1 now
where the time goes in v5:
time: 74.6 us; the launch traced here: 74.1 us
  starting transfers between devices  46.8 us (63%)
  waiting for transfers between devices  14.7 us (20%)
  Pallas kernels  5.08 us (7%)
  other arithmetic  3.7 us (5%)
  local copies, waits for them, and re-layouts  2.62 us (4%)
  matrix products  0.83 us (1%)
    ppermute x3, starting transfers between devices, shards(): sinks = sinks + lax.ppermute(sinks, axis, route)  11.9 us
    ppermute x3, waiting for transfers between devices, shards(): total += lax.ppermute(parts[distance], 'zl', route).astype(jnp.float32)  11.6 us
    ppermute x3, starting transfers between devices, shards(): total += lax.ppermute(parts[distance], 'zl', route).astype(jnp.float32)  11.6 us
    all_to_all x1, starting transfers between devices, shards(): lax.all_to_all(sent, 'y', 0, 0, axis_index_groups=[list(ORDER)], tiled=True)  8.73 us
    ppermute x3, starting transfers between devices, along_row(): sinks = sinks + lax.ppermute(sinks, axis, route)  8.29 us
    ppermute x1, starting transfers between devices, shards(): theirs = lax.ppermute(theirs, 'core', [(0, 1), (1, 0)])  4.98 us
    pallas_call x2, Pallas kernels, attend(): pl.pallas_call(functools.partial(attend_kernel, tok_rows=tok_rows, number...  3.24 us
    ppermute x3, waiting for transfers between devices, along_row(): sinks = sinks + lax.ppermute(sinks, axis, route)  2.15 us
  transfers between devices with their start and end apart: 12, of which 8 were waited for; matrix products, arithmetic and copies ran while one was open for 5% of the time, Pallas kernels for 2%

profile of v5, /device:TPU:1, one launch (start us, length us, event | category | flops | bytes accessed | tf_op | source)
XLA Modules:
  0.0 74.1 jit_solution(3178534419062861365)
XLA Ops:
  0.0 0.9 %pad_maximum_fusion.2.own_ref = bf16[2,192,128]{2,1,0:T(8,128)(2,1)S(1)} fusion(bf16[1,192,128]{2,1,0:T(8,128)(2,1)} %bitcast.23, bf16[1,192,128]{2,1,0:T(8,128)(2,1)} %bitcast.24), kind=kLoop, calls=%fused_computation.11 | loop fusion | flops 49152 | bytes 196608 | tf_op jit(solution)/shard_map/stack | solution.py:177
  0.9 4.8 %conditional.2 = (bf16[2,4,128]{2,1,0:T(4,128)(2,1)S(1)}) conditional(s32[]{:T(128)} %convert_element_type.28, () %tuple.21, (s32[]{:T(128)}, bf16[2,192,128]{2,1,0:T(8,128)(2,1)S(1)}) %tuple.22), branch_computations={%region_0.0_spmd, %region_1.2_spmd} | conditional | flops 2049 | bytes 18490 | solution.py:186
  0.9 4.0 %collective-permute-start.2 = (bf16[2,4,128]{2,1,0:T(4,128)(2,1)S(1)}, bf16[2,4,128]{2,1,0:T(4,128)(2,1)S(1)}, u32[]{:S(2)}, u32[]{:S(2)}) collective-permute-start(bf16[2,4,128]{2,1,0:T(4,128)(2,1)S(1)} %slice_select_fusion), channel_id=1, source_target_pairs={{0,8},{1,9},{2,10},{3,11},{4,12},{5,13},{6,14},{7,15}} | collective-permute-start | bytes 6152 | tf_op jit(solution)/shard_map/cond/branch_1_fun/ppermute | solution.py:183
  4.9 0.7 collective-permute-done.2
  5.7 1.3 %collective-permute-start.3 = (bf16[2,192,128]{2,1,0:T(8,128)(2,1)S(1)}, bf16[2,192,128]{2,1,0:T(8,128)(2,1)S(1)}, u32[]{:S(2)}, u32[]{:S(2)}) collective-permute-start(bf16[2,192,128]{2,1,0:T(8,128)(2,1)S(1)} %pad_maximum_fusion.2.own_ref), channel_id=1, source_target_pairs={{0,64},{8,72},{16,80},{24,88},{32,96},{40,104},{48,112},{56,120},{... | collective-permute-start | bytes 294920 | tf_op jit(solution)/shard_map/ppermute | solution.py:192
  7.0 5.7 %conditional.3 = (bf16[2,4,128]{2,1,0:T(4,128)(2,1)S(1)}) conditional(s32[]{:T(128)} %convert_element_type.28, bf16[2,4,128]{2,1,0:T(4,128)(2,1)S(1)} %get-tuple-element.51, bf16[2,4,128]{2,1,0:T(4,128)(2,1)S(1)} %get-tuple-element.51), branch_computations={%region_2.3_spmd, %region_3.4_spmd} | conditional | flops 2048 | bytes 28760 | solution.py:193
  7.0 3.0 %collective-permute-start = (bf16[2,4,128]{2,1,0:T(4,128)(2,1)S(1)}, bf16[2,4,128]{2,1,0:T(4,128)(2,1)S(1)}, u32[]{:S(2)}, u32[]{:S(2)}) collective-permute-start(bf16[2,4,128]{2,1,0:T(4,128)(2,1)S(1)} %param.3), channel_id=1, source_target_pairs={{0,56},{8,16},{1,57},{9,17},{2,58},{10,18},{3,59},{11,19},{4,60},{... | collective-permute-start | bytes 6152 | tf_op jit(solution)/shard_map/cond/branch_1_fun/ppermute | solution.py:183
  10.0 0.7 collective-permute-done
  10.7 1.3 %collective-permute-start.1 = (bf16[2,4,128]{2,1,0:T(4,128)(2,1)S(1)}, bf16[2,4,128]{2,1,0:T(4,128)(2,1)S(1)}, u32[]{:S(2)}, u32[]{:S(2)}) collective-permute-start(bf16[2,4,128]{2,1,0:T(4,128)(2,1)S(1)} %add.29), channel_id=1, source_target_pairs={{56,40},{0,48},{8,24},{16,32},{57,41},{1,49},{9,25},{17,33},{58,42... | collective-permute-start | bytes 6152 | tf_op jit(solution)/shard_map/cond/branch_1_fun/ppermute | solution.py:183
  12.0 0.7 collective-permute-done.1
  12.7 1.0 %pack.1 = bf16[8,2,192,128]{3,2,1,0:T(8,128)(2,1)} custom-call(bf16[2,192,128]{2,1,0:T(8,128)(2,1)S(1)} %pad_maximum_fusion.2.own_ref, bf16[2,192,128]{2,1,0:T(8,128)(2,1)S(1)} %collective-permute-done.3.before_ref), custom_call_target="tpu_custom_call" | custom-call | tf_op jit(solution)/shard_map/pack/pallas_call | solution.py:51
  13.7 8.7 %all-to-all-start = ((bf16[8,2,192,128]{3,2,1,0:T(8,128)(2,1)}), bf16[8,2,192,128]{3,2,1,0:T(8,128)(2,1)S(1)}, u32[]{:S(2)}, u32[]{:S(2)}) async-start(bf16[8,2,192,128]{3,2,1,0:T(8,128)(2,1)} %pack.1), calls=%async_computation | async-start | bytes 1572864 | tf_op jit(solution)/shard_map/all_to_all | solution.py:198
  22.4 1.3 %collective-permute-start.4 = (bf16[2,4,128]{2,1,0:T(4,128)(2,1)S(1)}, bf16[2,4,128]{2,1,0:T(4,128)(2,1)S(1)}, u32[]{:S(2)}, u32[]{:S(2)}) collective-permute-start(bf16[2,4,128]{2,1,0:T(4,128)(2,1)S(1)} %get-tuple-element.52), channel_id=1, source_target_pairs={{0,64},{8,72},{16,80},{24,88},{32,96},{40,104},{48,112},{56,120},{... | collective-permute-start | bytes 6152 | tf_op jit(solution)/shard_map/ppermute | solution.py:205
  23.7 0.7 broadcast_multiply_fusion
  24.4 0.7 %concatenate.6 = s32[13]{0:T(128)S(1)} concatenate(s32[1]{0:T(128)} %bitcast, s32[1]{0:T(128)} %bitcast.1, s32[1]{0:T(128)} %bitcast.2, s32[1]{0:T(128)} %bitcast.3, s32[1]{0:T(128)} %bitcast.4, s32[4]{0:T(128)} %param.14, s32[4]{0:T(128)} %param.15), dimensions={0} | concatenate | bytes 104 | tf_op jit(solution)/shard_map/concatenate | solution.py:218
  25.2 4.4 %collective-permute-start.5 = (bf16[2,4,128]{2,1,0:T(4,128)(2,1)S(1)}, bf16[2,4,128]{2,1,0:T(4,128)(2,1)S(1)}, u32[]{:S(2)}, u32[]{:S(2)}) collective-permute-start(bf16[2,4,128]{2,1,0:T(4,128)(2,1)S(1)} %add.51), channel_id=1, source_target_pairs={{0,192},{64,128},{8,200},{72,136},{16,208},{80,144},{24,216},{88,1... | collective-permute-start | bytes 6152 | tf_op jit(solution)/shard_map/ppermute | solution.py:205
  29.6 1.0 %fusion.4 = (bf16[2,1,2,24,4,128]{5,4,3,2,1,0:T(4,128)(2,1)S(1)}, bf16[2,1,2,24,4,128]{5,4,3,2,1,0:T(4,128)(2,1)S(1)}) fusion(bf16[2,2,2,24,4,128]{5,4,3,2,1,0:T(4,128)(2,1)} %bitcast.18), kind=kLoop, calls=%fused_computation.14 | loop fusion | bytes 393216 | tf_op jit(solution)/shard_map/slice | solution.py:213
  30.6 1.1 %pad_maximum_fusion = (bf16[2,2,2,24,4,128]{5,4,3,2,1,0:T(4,128)(2,1)S(1)}, bf16[2,2,2,24,4,128]{5,4,3,2,1,0:T(4,128)(2,1)S(1)}) fusion(bf16[2,1,2,24,4,128]{5,4,3,2,1,0:T(4,128)(2,1)S(1)} %get-tuple-element.50, bf16[2,1,2,24,4,128]{5,4,3,2,1,0:T(4,128)(2,1)S(1)} %get-tuple-element.49, bf16[2,2,2,24,4,128]{5,4,3,2,1,0:T(4,128)(2,1)} %bitcast.19, pred[]{:T(512)S(6)} %eq.16), kind=kLoop, calls=%fused_computation.5 | loop fusion | flops 196608 | bytes 786433 | tf_op jit(solution)/shard_map/stack | solution.py:213
  32.1 6.2 %collective-permute-start.6 = (bf16[2,4,128]{2,1,0:T(4,128)(2,1)S(1)}, bf16[2,4,128]{2,1,0:T(4,128)(2,1)S(1)}, u32[]{:S(2)}, u32[]{:S(2)}) collective-permute-start(bf16[2,4,128]{2,1,0:T(4,128)(2,1)S(1)} %add.52), channel_id=1, source_target_pairs={{0,256},{1,257},{2,258},{3,259},{4,260},{5,261},{6,262},{7,263},{8... | collective-permute-start | bytes 6152 | tf_op jit(solution)/shard_map/ppermute | solution.py:205
  38.4 0.7 collective-permute-done.6
  39.2 1.6 %attend.3 = bf16[96,512]{1,0:T(8,128)(2,1)S(1)} custom-call(s32[16,128]{1,0:T(8,128)S(1)} %broadcast_in_dim.8.table, f32[8,128]{1,0:T(8,128)S(1)} %broadcast_in_dim.9.bias, bf16[2,4,96,128]{3,2,1,0:T(8,128)(2,1)S(1)} %bitcast.16, bf16[8,2,192,128]{3,2,1,0:T(8,128)(2,1)S(1)} %all-to-all-done.halo_ref, bf16[2,256,128]{2,1,0:T(8,128)(2,1)S(1)} %fusion.2.near_ref), custom_call_target="tpu_custom_call" | custom-call | flops 2818572288 | bytes 786432 | tf_op jit(solution)/shard_map/attend/pallas_call | solution.py:123
  41.4 0.8 %convolution_convert_fusion = bf16[96,4096]{1,0:T(8,128)(2,1)S(1)} fusion(bf16[96,512]{1,0:T(8,128)(2,1)S(1)} %attend.3, bf16[512,4096]{1,0:T(8,128)(2,1)S(1)} %copy-done), kind=kOutput, calls=%fused_computation.1 | convolution fusion | flops 403046400 | bytes 5079040 | tf_op jit(solution)/shard_map/dot_general | solution.py:224
  42.2 5.0 %collective-permute-start.7 = (bf16[96,4096]{1,0:T(8,128)(2,1)S(1)}, bf16[96,4096]{1,0:T(8,128)(2,1)S(1)}, u32[]{:S(2)}, u32[]{:S(2)}) collective-permute-start(bf16[96,4096]{1,0:T(8,128)(2,1)S(1)} %convolution_convert_fusion), channel_id=1, source_target_pairs={{0,1},{1,0},{2,3},{3,2},{4,5},{5,4},{6,7},{7,6},{8,9},{9,8},{10,11... | collective-permute-start | bytes 2359304 | tf_op jit(solution)/shard_map/ppermute | solution.py:225
  47.2 1.6 %attend.2.rows_ref = bf16[96,512]{1,0:T(8,128)(2,1)S(1)} custom-call(s32[16,128]{1,0:T(8,128)S(1)} %broadcast_in_dim.8.table, f32[8,128]{1,0:T(8,128)S(1)} %broadcast_in_dim.9.bias, bf16[2,4,96,128]{3,2,1,0:T(8,128)(2,1)S(1)} %bitcast.17, bf16[8,2,192,128]{3,2,1,0:T(8,128)(2,1)S(1)} %all-to-all-done.halo_ref, bf16[2,256,128]{2,1,0:T(8,128)(2,1)S(1)} %fusion.2.near_ref), custom_call_target="tpu_custom_call" | custom-call | flops 2818572288 | bytes 786432 | tf_op jit(solution)/shard_map/attend/pallas_call | solution.py:123
  49.1 0.9 %project.1 = (bf16[24,4096]{1,0:T(8,128)(2,1)S(1)}, bf16[24,4096]{1,0:T(8,128)(2,1)S(1)}, bf16[24,4096]{1,0:T(8,128)(2,1)S(1)}, bf16[24,4096]{1,0:T(8,128)(2,1)S(1)}) custom-call(bf16[96,512]{1,0:T(8,128)(2,1)S(1)} %attend.2.rows_ref, bf16[512,4096]{1,0:T(8,128)(2,1)S(1)} %copy-done, bf16[96,4096]{1,0:T(8,128)(2,1)S(1)} %collective-permute-done.7.theirs_ref), custom_call_target="tpu_custom_call" | custom-call | flops 402653184 | bytes 4194304 | tf_op jit(solution)/shard_map/project/pallas_call | solution.py:158
  50.0 7.5 %collective-permute-start.10 = (bf16[24,4096]{1,0:T(8,128)(2,1)S(1)}, bf16[24,4096]{1,0:T(8,128)(2,1)S(1)}, u32[]{:S(2)}, u32[]{:S(2)}) collective-permute-start(bf16[24,4096]{1,0:T(8,128)(2,1)S(1)} %get-tuple-element.44), channel_id=1, source_target_pairs={{0,6},{2,4},{4,2},{6,0},{1,7},{3,5},{5,3},{7,1},{8,14},{10,12},{12... | collective-permute-start | bytes 589832 | tf_op jit(solution)/shard_map/ppermute | solution.py:231
  57.5 1.9 %collective-permute-start.9 = (bf16[24,4096]{1,0:T(8,128)(2,1)S(1)}, bf16[24,4096]{1,0:T(8,128)(2,1)S(1)}, u32[]{:S(2)}, u32[]{:S(2)}) collective-permute-start(bf16[24,4096]{1,0:T(8,128)(2,1)S(1)} %get-tuple-element.43), channel_id=1, source_target_pairs={{0,2},{2,0},{4,6},{6,4},{1,3},{3,1},{5,7},{7,5},{8,10},{10,8},{12,... | collective-permute-start | bytes 589832 | tf_op jit(solution)/shard_map/ppermute | solution.py:231
  59.4 2.2 %collective-permute-start.8 = (bf16[24,4096]{1,0:T(8,128)(2,1)S(1)}, bf16[24,4096]{1,0:T(8,128)(2,1)S(1)}, u32[]{:S(2)}, u32[]{:S(2)}) collective-permute-start(bf16[24,4096]{1,0:T(8,128)(2,1)S(1)} %get-tuple-element.42), channel_id=1, source_target_pairs={{0,4},{2,6},{4,0},{6,2},{1,5},{3,7},{5,1},{7,3},{8,12},{10,14},{12... | collective-permute-start | bytes 589832 | tf_op jit(solution)/shard_map/ppermute | solution.py:231
  61.6 0.8 %collective-permute-done.10 = bf16[24,4096]{1,0:T(8,128)(2,1)S(1)} collective-permute-done((bf16[24,4096]{1,0:T(8,128)(2,1)S(1)}, bf16[24,4096]{1,0:T(8,128)(2,1)S(1)}, u32[]{:S(2)}, u32[]{:S(2)}) %collective-permute-start.10) | collective-permute-done | bytes 196640 | tf_op jit(solution)/shard_map/ppermute | solution.py:231
  62.4 6.3 %collective-permute-done.9 = bf16[24,4096]{1,0:T(8,128)(2,1)S(1)} collective-permute-done((bf16[24,4096]{1,0:T(8,128)(2,1)S(1)}, bf16[24,4096]{1,0:T(8,128)(2,1)S(1)}, u32[]{:S(2)}, u32[]{:S(2)}) %collective-permute-start.9) | collective-permute-done | bytes 196640 | tf_op jit(solution)/shard_map/ppermute | solution.py:231
  68.8 4.5 %collective-permute-done.8 = bf16[24,4096]{1,0:T(8,128)(2,1)S(1)} collective-permute-done((bf16[24,4096]{1,0:T(8,128)(2,1)S(1)}, bf16[24,4096]{1,0:T(8,128)(2,1)S(1)}, u32[]{:S(2)}, u32[]{:S(2)}) %collective-permute-start.8) | collective-permute-done | bytes 196640 | tf_op jit(solution)/shard_map/ppermute | solution.py:231
  73.3 0.8 %add_convert_fusion = bf16[24,4096]{1,0:T(8,128)(2,1)} fusion(bf16[24,4096]{1,0:T(8,128)(2,1)S(1)} %collective-permute-done.10, bf16[24,4096]{1,0:T(8,128)(2,1)S(1)} %collective-permute-done.9, bf16[24,4096]{1,0:T(8,128)(2,1)S(1)} %collective-permute-done.8, bf16[24,4096]{1,0:T(8,128)(2,1)S(1)} %get-tuple-element.41), kind=kLoop, calls=%fused_computation.2 | loop fusion | flops 786432 | bytes 983040 | tf_op jit(solution)/shard_map/convert_element_type | solution.py:232
  (26 shorter events, 1.4 us)
Async XLA Ops:
  0.0 38.3 %copy-start.1 = (bf16[192,4,128]{2,1,0:T(4,128)(2,1)S(1)}, bf16[192,4,128]{2,1,0:T(4,128)(2,1)}, u32[]{:S(2)}) copy-start(bf16[192,4,128]{2,1,0:T(4,128)(2,1)} %param.11) | copy-start | bytes 589828
  0.9 4.7 %collective-permute-start.2 = (bf16[2,4,128]{2,1,0:T(4,128)(2,1)S(1)}, bf16[2,4,128]{2,1,0:T(4,128)(2,1)S(1)}, u32[]{:S(2)}, u32[]{:S(2)}) collective-permute-start(bf16[2,4,128]{2,1,0:T(4,128)(2,1)S(1)} %slice_select_fusion), channel_id=1, source_target_pairs={{0,8},{1,9},{2,10},{3,11},{4,12},{5,13},{6,14},{7,15}} | collective-permute-start | bytes 6152 | tf_op jit(solution)/shard_map/cond/branch_1_fun/ppermute | solution.py:183
  5.7 7.1 %collective-permute-start.3 = (bf16[2,192,128]{2,1,0:T(8,128)(2,1)S(1)}, bf16[2,192,128]{2,1,0:T(8,128)(2,1)S(1)}, u32[]{:S(2)}, u32[]{:S(2)}) collective-permute-start(bf16[2,192,128]{2,1,0:T(8,128)(2,1)S(1)} %pad_maximum_fusion.2.own_ref), channel_id=1, source_target_pairs={{0,64},{8,72},{16,80},{24,88},{32,96},{40,104},{48,112},{56,120},{... | collective-permute-start | bytes 294920 | tf_op jit(solution)/shard_map/ppermute | solution.py:192
  7.0 3.7 %collective-permute-start = (bf16[2,4,128]{2,1,0:T(4,128)(2,1)S(1)}, bf16[2,4,128]{2,1,0:T(4,128)(2,1)S(1)}, u32[]{:S(2)}, u32[]{:S(2)}) collective-permute-start(bf16[2,4,128]{2,1,0:T(4,128)(2,1)S(1)} %param.3), channel_id=1, source_target_pairs={{0,56},{8,16},{1,57},{9,17},{2,58},{10,18},{3,59},{11,19},{4,60},{... | collective-permute-start | bytes 6152 | tf_op jit(solution)/shard_map/cond/branch_1_fun/ppermute | solution.py:183
  10.7 2.0 %collective-permute-start.1 = (bf16[2,4,128]{2,1,0:T(4,128)(2,1)S(1)}, bf16[2,4,128]{2,1,0:T(4,128)(2,1)S(1)}, u32[]{:S(2)}, u32[]{:S(2)}) collective-permute-start(bf16[2,4,128]{2,1,0:T(4,128)(2,1)S(1)} %add.29), channel_id=1, source_target_pairs={{56,40},{0,48},{8,24},{16,32},{57,41},{1,49},{9,25},{17,33},{58,42... | collective-permute-start | bytes 6152 | tf_op jit(solution)/shard_map/cond/branch_1_fun/ppermute | solution.py:183
  13.7 25.4 %all-to-all-start = ((bf16[8,2,192,128]{3,2,1,0:T(8,128)(2,1)}), bf16[8,2,192,128]{3,2,1,0:T(8,128)(2,1)S(1)}, u32[]{:S(2)}, u32[]{:S(2)}) async-start(bf16[8,2,192,128]{3,2,1,0:T(8,128)(2,1)} %pack.1), calls=%async_computation | async-start | bytes 1572864 | tf_op jit(solution)/shard_map/all_to_all | solution.py:198
  22.4 2.7 %collective-permute-start.4 = (bf16[2,4,128]{2,1,0:T(4,128)(2,1)S(1)}, bf16[2,4,128]{2,1,0:T(4,128)(2,1)S(1)}, u32[]{:S(2)}, u32[]{:S(2)}) collective-permute-start(bf16[2,4,128]{2,1,0:T(4,128)(2,1)S(1)} %get-tuple-element.52), channel_id=1, source_target_pairs={{0,64},{8,72},{16,80},{24,88},{32,96},{40,104},{48,112},{56,120},{... | collective-permute-start | bytes 6152 | tf_op jit(solution)/shard_map/ppermute | solution.py:205
  25.2 6.9 %collective-permute-start.5 = (bf16[2,4,128]{2,1,0:T(4,128)(2,1)S(1)}, bf16[2,4,128]{2,1,0:T(4,128)(2,1)S(1)}, u32[]{:S(2)}, u32[]{:S(2)}) collective-permute-start(bf16[2,4,128]{2,1,0:T(4,128)(2,1)S(1)} %add.51), channel_id=1, source_target_pairs={{0,192},{64,128},{8,200},{72,136},{16,208},{80,144},{24,216},{88,1... | collective-permute-start | bytes 6152 | tf_op jit(solution)/shard_map/ppermute | solution.py:205
  32.1 6.9 %collective-permute-start.6 = (bf16[2,4,128]{2,1,0:T(4,128)(2,1)S(1)}, bf16[2,4,128]{2,1,0:T(4,128)(2,1)S(1)}, u32[]{:S(2)}, u32[]{:S(2)}) collective-permute-start(bf16[2,4,128]{2,1,0:T(4,128)(2,1)S(1)} %add.52), channel_id=1, source_target_pairs={{0,256},{1,257},{2,258},{3,259},{4,260},{5,261},{6,262},{7,263},{8... | collective-permute-start | bytes 6152 | tf_op jit(solution)/shard_map/ppermute | solution.py:205
  39.2 2.2 %copy-start = (bf16[512,4096]{1,0:T(8,128)(2,1)S(1)}, bf16[512,4096]{1,0:T(8,128)(2,1)}, u32[]{:S(2)}) copy-start(bf16[512,4096]{1,0:T(8,128)(2,1)} %weight_ref.1) | copy-start | bytes 12582916
  42.2 6.9 %collective-permute-start.7 = (bf16[96,4096]{1,0:T(8,128)(2,1)S(1)}, bf16[96,4096]{1,0:T(8,128)(2,1)S(1)}, u32[]{:S(2)}, u32[]{:S(2)}) collective-permute-start(bf16[96,4096]{1,0:T(8,128)(2,1)S(1)} %convolution_convert_fusion), channel_id=1, source_target_pairs={{0,1},{1,0},{2,3},{3,2},{4,5},{5,4},{6,7},{7,6},{8,9},{9,8},{10,11... | collective-permute-start | bytes 2359304 | tf_op jit(solution)/shard_map/ppermute | solution.py:225
  50.0 12.5 %collective-permute-start.10 = (bf16[24,4096]{1,0:T(8,128)(2,1)S(1)}, bf16[24,4096]{1,0:T(8,128)(2,1)S(1)}, u32[]{:S(2)}, u32[]{:S(2)}) collective-permute-start(bf16[24,4096]{1,0:T(8,128)(2,1)S(1)} %get-tuple-element.44), channel_id=1, source_target_pairs={{0,6},{2,4},{4,2},{6,0},{1,7},{3,5},{5,3},{7,1},{8,14},{10,12},{12... | collective-permute-start | bytes 589832 | tf_op jit(solution)/shard_map/ppermute | solution.py:231
  57.5 11.3 %collective-permute-start.9 = (bf16[24,4096]{1,0:T(8,128)(2,1)S(1)}, bf16[24,4096]{1,0:T(8,128)(2,1)S(1)}, u32[]{:S(2)}, u32[]{:S(2)}) collective-permute-start(bf16[24,4096]{1,0:T(8,128)(2,1)S(1)} %get-tuple-element.43), channel_id=1, source_target_pairs={{0,2},{2,0},{4,6},{6,4},{1,3},{3,1},{5,7},{7,5},{8,10},{10,8},{12,... | collective-permute-start | bytes 589832 | tf_op jit(solution)/shard_map/ppermute | solution.py:231
  59.4 13.8 %collective-permute-start.8 = (bf16[24,4096]{1,0:T(8,128)(2,1)S(1)}, bf16[24,4096]{1,0:T(8,128)(2,1)S(1)}, u32[]{:S(2)}, u32[]{:S(2)}) collective-permute-start(bf16[24,4096]{1,0:T(8,128)(2,1)S(1)} %get-tuple-element.42), channel_id=1, source_target_pairs={{0,4},{2,6},{4,0},{6,2},{1,5},{3,7},{5,1},{7,3},{8,12},{10,14},{12... | collective-permute-start | bytes 589832 | tf_op jit(solution)/shard_map/ppermute | solution.py:231
